TPU v7x, 32 devices: a whole 2x2x4 slice. The times are simulated.
32 devices in a mesh: batch: 4 (over x, core), seq: 8 (over z, y).
Axes of the slice: x: 2, y: 2, z: 4, core: 2. Of those that a mesh axis runs over, the one named last changes fastest.
Arguments:
- tokens: bfloat16 [16, 2048, 768], P('batch', 'seq'), may hold values from -6 to 6
- prompts: float32 [50, 768], replicated, may hold values from -6 to 6
- image_id: int32 [16, 2048], P('batch'), may hold values from 0 to 8, as said below
- prompt_slot: int32 [16, 2048], P('batch', 'seq'), may hold values from 0 to 50, as said below
- ln1_gain: float32 [768], replicated, may hold values from 0.5 to 1.5
- ln1_bias: float32 [768], replicated, may hold values from -1.8 to 1.8
- w_qkv: bfloat16 [768, 2304], replicated, may hold values from -0.21875 to 0.21875
- bias_qv: float32 [1536], replicated, may hold values from -1.8 to 1.8
- w_out: bfloat16 [768, 768], replicated, may hold values from -0.875 to 0.875
- bias_out: float32 [768], replicated, may hold values from -1.8 to 1.8
- ln2_gain: float32 [768], replicated, may hold values from 0.5 to 1.5
- ln2_bias: float32 [768], replicated, may hold values from -1.8 to 1.8
- w_up: bfloat16 [768, 3072], replicated, may hold values from -0.21875 to 0.21875
- bias_up: float32 [3072], replicated, may hold values from -1.8 to 1.8
- w_down: bfloat16 [3072, 768], replicated, may hold values from -0.109375 to 0.109375
- bias_down: float32 [768], replicated, may hold values from -1.8 to 1.8
- cotangent: bfloat16 [16, 2048, 768], P('batch', 'seq'), may hold values from -6 to 6
Outputs:
- output: bfloat16 [16, 2048, 768], P('batch', 'seq')
- token_gradient: bfloat16 [16, 2048, 768], P('batch', 'seq')
- prompt_gradient: float32 [50, 768], replicated
Inputs may be any that keep to these rules, and one draw needn't show every extreme that they name: `image_id`: each row holds 8 runs of 247 consecutive positions with ids 0 to 7 in order; all other positions (padding, some before, between or after the runs) have id 8. `prompt_slot`: within each run of image_id, the first position is the class token, the next 50 carry slots 0 to 49 in order; class tokens, patches and padding carry 50.
All inputs are finite; a program needn't handle non-finite values.
Results may differ from a plain program's by a relative error of at most 0.012.
Values may be sent and summed in bfloat16 or wider, within the bound.
A program may use at most 384 MiB of HBM per device.

v0:
```python
import jax
import jax.numpy as jnp
from jax import lax
from jax.sharding import PartitionSpec as P

ATTENTION_HEADS = 12
HEAD_FEATURES = 64
PROMPTS = 50
IMAGES_PER_ROW = 8
IMAGE_TOKENS = 247


def passed_along(block, axis, distance):
    devices = range(lax.axis_size(axis))
    route = [(i - distance, i) for i in devices if i - distance in devices]
    return lax.ppermute(block, axis, route)


def normalize(value_rows):
    mean = jnp.mean(value_rows, axis=-1, keepdims=True)
    centered = value_rows - mean
    inverse = lax.rsqrt(jnp.mean(centered * centered, axis=-1, keepdims=True) + 1e-06)
    return (centered * inverse, inverse)


def norm_back(grad_in, normal_draws, inverse, gain):
    scaled = grad_in * gain
    return inverse * (
        scaled
        - jnp.mean(scaled, axis=-1, keepdims=True)
        - normal_draws * jnp.mean(scaled * normal_draws, axis=-1, keepdims=True)
    )


def block_rows(rows, span):
    group = min(rows, max(1, 512 // span))
    while rows % group:
        group = group - 1
    return group


def masked_scores(query_rows, key_rows, query_ids, key_ids, own_pos, key_pos):
    scores = jnp.einsum(
        "gqhd,gkhd->ghqk", query_rows, key_rows, preferred_element_type=jnp.float32
    ) * HEAD_FEATURES ** (-0.5)
    same_image = (query_ids[:, :, None] == key_ids[:, None, :]) & (query_ids < IMAGES_PER_ROW)[
        :, :, None
    ]
    permitted_mask = same_image | (own_pos[:, None] == key_pos[None, :])[None]
    return jnp.where(permitted_mask[:, None], scores, -1e30)


def body(
    tokens,
    prompts,
    image_id,
    prompt_slot,
    ln1_gain,
    ln1_bias,
    w_qkv,
    bias_qv,
    w_out,
    bias_out,
    ln2_gain,
    ln2_bias,
    w_up,
    bias_up,
    w_down,
    bias_down,
    cotangent,
):
    rows, span, width = tokens.shape
    length = image_id.shape[1]
    start = lax.axis_index("seq") * span
    own_ids = lax.dynamic_slice_in_dim(image_id, start, span, 1)
    own_pos = start + jnp.arange(span, dtype=jnp.int32)
    valid = (own_ids < IMAGES_PER_ROW).astype(jnp.float32)
    one_hot = (prompt_slot[..., None] == jnp.arange(PROMPTS, dtype=jnp.int32)).astype(jnp.float32)
    placed = jnp.einsum("rsn,nd->rsd", one_hot, prompts, precision=lax.Precision.HIGHEST)
    is_prompt = (prompt_slot < PROMPTS)[..., None]
    inserted = jnp.where(is_prompt, placed, tokens.astype(jnp.float32))
    normal1, inverse1 = normalize(inserted)
    normed1 = (normal1 * ln1_gain + ln1_bias).astype(jnp.bfloat16)
    bias_three = jnp.concatenate(
        [bias_qv[:width], jnp.zeros((width,), jnp.float32), bias_qv[width:]]
    )
    query_key_value = (
        jnp.einsum("rsd,de->rse", normed1, w_qkv, preferred_element_type=jnp.float32) + bias_three
    ).astype(jnp.bfloat16)
    query_rows = query_key_value[..., :width]
    key_own = query_key_value[..., width : 2 * width]
    value_own = query_key_value[..., 2 * width :]
    reach = (IMAGE_TOKENS - 2 + span) // span
    offsets = list(range(-reach, reach + 1))
    key_parts = []
    value_parts = []
    for offset in offsets:
        if offset == 0:
            fetched_key, fetched_value = (key_own, value_own)
        else:
            fetched_key, fetched_value = passed_along((key_own, value_own), "seq", -offset)
        key_parts.append(fetched_key)
        value_parts.append(fetched_value)
    key_rows = jnp.concatenate(key_parts, axis=1)
    value_rows = jnp.concatenate(value_parts, axis=1)
    raw_pos = jnp.concatenate(
        [start + offset * span + jnp.arange(span, dtype=jnp.int32) for offset in offsets]
    )
    in_row = (raw_pos >= 0) & (raw_pos < length)
    taken = jnp.take(image_id, jnp.clip(raw_pos, 0, length - 1), axis=1)
    key_ids = jnp.where(in_row[None, :], taken, -1)
    key_pos = jnp.where(in_row, raw_pos, -1)
    key_count = key_rows.shape[1]
    group = block_rows(rows, span)

    def grouped(array):
        return array.reshape((rows // group, group) + array.shape[1:])

    query_heads = grouped(query_rows.reshape(rows, span, ATTENTION_HEADS, HEAD_FEATURES))
    key_heads = grouped(key_rows.reshape(rows, key_count, ATTENTION_HEADS, HEAD_FEATURES))
    value_heads = grouped(value_rows.reshape(rows, key_count, ATTENTION_HEADS, HEAD_FEATURES))
    query_ids = grouped(own_ids)
    grouped_key_ids = grouped(key_ids)

    def forward_block(inputs):
        query_blk, key_blk, value_blk, qid_blk, kid_blk = inputs
        scores = masked_scores(query_blk, key_blk, qid_blk, kid_blk, own_pos, key_pos)
        row_top = jnp.max(scores, axis=-1, keepdims=True)
        total = jnp.sum(jnp.exp(scores - row_top), axis=-1, keepdims=True)
        log_total = row_top + jnp.log(total)
        attention_weights = jnp.exp(scores - log_total).astype(jnp.bfloat16)
        attention_output = jnp.einsum(
            "vbta,vabj->vtbj", attention_weights, value_blk, preferred_element_type=jnp.float32
        )
        return (attention_output.astype(jnp.bfloat16), log_total[..., 0])

    attention_output, log_totals = lax.map(
        forward_block, (query_heads, key_heads, value_heads, query_ids, grouped_key_ids)
    )
    attention_output = attention_output.reshape(rows, span, width)
    hidden1 = (
        inserted
        + jnp.einsum("rsd,de->rse", attention_output, w_out, preferred_element_type=jnp.float32)
        + bias_out
    )
    normal2, inverse2 = normalize(hidden1)
    normed2 = (normal2 * ln2_gain + ln2_bias).astype(jnp.bfloat16)
    upper = jnp.einsum("rsd,df->rsf", normed2, w_up, preferred_element_type=jnp.float32) + bias_up
    activated, gelu_pull = jax.vjp(lambda inner: jax.nn.gelu(inner, approximate=False), upper)
    activated = activated.astype(jnp.bfloat16)
    output = (
        hidden1
        + jnp.einsum("rsf,fd->rsd", activated, w_down, preferred_element_type=jnp.float32)
        + bias_down
    ).astype(jnp.bfloat16)
    out_grad = cotangent.astype(jnp.float32) * valid[..., None]
    act_grad = jnp.einsum(
        "rsd,fd->rsf", out_grad.astype(jnp.bfloat16), w_down, preferred_element_type=jnp.float32
    )
    upper_grad = gelu_pull(act_grad)[0].astype(jnp.bfloat16)
    normed2_grad = jnp.einsum("rsf,df->rsd", upper_grad, w_up, preferred_element_type=jnp.float32)
    hidden1_grad = out_grad + norm_back(normed2_grad, normal2, inverse2, ln2_gain)
    attended_grad = jnp.einsum(
        "rse,de->rsd", hidden1_grad.astype(jnp.bfloat16), w_out, preferred_element_type=jnp.float32
    ).astype(jnp.bfloat16)
    attended_grad = grouped(attended_grad.reshape(rows, span, ATTENTION_HEADS, HEAD_FEATURES))

    def backward_block(inputs):
        query_blk, key_blk, value_blk, qid_blk, kid_blk, total_blk, grad_blk = inputs
        scores = masked_scores(query_blk, key_blk, qid_blk, kid_blk, own_pos, key_pos)
        attention_weights = jnp.exp(scores - total_blk[..., None])
        value_grad = jnp.einsum(
            "ghqk,gqhd->gkhd",
            attention_weights.astype(jnp.bfloat16),
            grad_blk,
            preferred_element_type=jnp.float32,
        )
        prob_grad = jnp.einsum(
            "gqhd,gkhd->ghqk", grad_blk, value_blk, preferred_element_type=jnp.float32
        )
        inner = jnp.sum(attention_weights * prob_grad, axis=-1, keepdims=True)
        score_grad = (attention_weights * (prob_grad - inner)).astype(jnp.bfloat16)
        query_grad = jnp.einsum(
            "vbta,vabj->vtbj", score_grad, key_blk, preferred_element_type=jnp.float32
        ) * HEAD_FEATURES ** (-0.5)
        key_grad = jnp.einsum(
            "ghqk,gqhd->gkhd", score_grad, query_blk, preferred_element_type=jnp.float32
        ) * HEAD_FEATURES ** (-0.5)
        return (query_grad, key_grad, value_grad)

    query_grad, key_grad, value_grad = lax.map(
        backward_block,
        (
            query_heads,
            key_heads,
            value_heads,
            query_ids,
            grouped_key_ids,
            log_totals,
            attended_grad,
        ),
    )
    query_grad = query_grad.reshape(rows, span, width)
    key_grad = key_grad.reshape(rows, key_count, width)
    value_grad = value_grad.reshape(rows, key_count, width)
    key_total = key_grad[:, reach * span : (reach + 1) * span]
    value_total = value_grad[:, reach * span : (reach + 1) * span]
    for offset in range(-reach, reach + 1):
        if offset != 0:
            first = (offset + reach) * span
            back_key, back_value = (
                passed_along(
                    key_grad[:, first : first + span].astype(jnp.bfloat16), "seq", offset
                ).astype(jnp.float32),
                passed_along(
                    value_grad[:, first : first + span].astype(jnp.bfloat16), "seq", offset
                ).astype(jnp.float32),
            )
            key_total = key_total + back_key
            value_total = value_total + back_value
    qkv_grad = jnp.concatenate([query_grad, key_total, value_total], axis=-1).astype(jnp.bfloat16)
    normed1_grad = jnp.einsum("rse,de->rsd", qkv_grad, w_qkv, preferred_element_type=jnp.float32)
    inserted_grad = hidden1_grad + norm_back(normed1_grad, normal1, inverse1, ln1_gain)
    token_gradient = jnp.where(is_prompt, 0.0, inserted_grad).astype(jnp.bfloat16)
    prompt_part = jnp.einsum("rsn,rsd->nd", one_hot, inserted_grad, precision=lax.Precision.HIGHEST)
    prompt_gradient = lax.psum(prompt_part, ("batch", "seq"))
    return (output, token_gradient, prompt_gradient)


def solution(mesh):
    in_specs = (
        P("batch", "seq", None),
        P(),
        P("batch", None),
        P("batch", "seq"),
        P(),
        P(),
        P(),
        P(),
        P(),
        P(),
        P(),
        P(),
        P(),
        P(),
        P(),
        P(),
        P("batch", "seq", None),
    )
    out_specs = (P("batch", "seq", None), P("batch", "seq", None), P())
    return jax.shard_map(body, mesh=mesh, in_specs=in_specs, out_specs=out_specs, check_vma=False)
```

profile of v0, /device:TPU:0, one launch (start us, length us, event | category | flops | bytes accessed | tf_op | source)
XLA Modules:
  0.0 713.7 jit_solution(10487192284243288981)
XLA Ops:
  9.6 3.3 fusion.128
  13.5 4.3 add_convert_fusion.1
  17.9 2.3 fusion.126
  21.5 6.7 collective-permute-start.2
  29.5 5.9 collective-permute-start
  35.4 2.1 copy.34
  38.8 3.5 gather_fusion
  44.0 2.6 copy.36
  48.7 12.0 %collective-permute-done.3 = bf16[4,256,768]{2,1,0:T(8,128)(2,1)} collective-permute-done((bf16[4,256,768]{2,1,0:T(8,128)(2,1)}, bf16[4,256,768]{2,1,0:T(8,128)(2,1)}, u32[]{:S(2)}, u32[]{:S(2)}) %collective-permute-start.3) | collective-permute-done | bytes 1572896 | tf_op jit(solution)/shard_map/ppermute | solution.py:16
  60.6 66.8 %collective-permute-done.2 = bf16[4,256,768]{2,1,0:T(8,128)(2,1)} collective-permute-done((bf16[4,256,768]{2,1,0:T(8,128)(2,1)}, bf16[4,256,768]{2,1,0:T(8,128)(2,1)}, u32[]{:S(2)}, u32[]{:S(2)}) %collective-permute-start.2) | collective-permute-done | bytes 1572896 | tf_op jit(solution)/shard_map/ppermute | solution.py:16
  127.4 3.9 pad_maximum_fusion.1
  131.4 6.6 copy.37
  138.0 23.1 %collective-permute-done = bf16[4,256,768]{2,1,0:T(8,128)(2,1)} collective-permute-done((bf16[4,256,768]{2,1,0:T(8,128)(2,1)}, bf16[4,256,768]{2,1,0:T(8,128)(2,1)}, u32[]{:S(2)}, u32[]{:S(2)}) %collective-permute-start) | collective-permute-done | bytes 1572896 | tf_op jit(solution)/shard_map/ppermute | solution.py:16
  161.1 3.9 pad_maximum_fusion
  165.0 6.6 copy.33
  171.6 47.5 %while.28 = (s32[]{:T(128)}, bf16[2,2,256,12,64]{2,4,3,1,0:T(8,128)(2,1)}, f32[2,2,12,256]{3,2,1,0:T(8,128)}, bf16[2,2,768,12,64]{2,4,3,1,0:T(8,128)(2,1)}, s32[...) while((s32[]{:T(128)}, ...), condition=%wide.region_5.6_spmd.clone, body=%wide.region_2.5_spmd.clone.sunk | while | flops 1261628160 | bytes 141033712 | solution.py:137
  172.8 5.4 fusion.151
  178.2 4.6 exponential_reduce_fusion.2
  182.8 1.8 copy-done.2
  184.7 10.4 %fusion.152 = bf16[2,2,256,12,64]{2,4,3,1,0:T(8,128)(2,1)} fusion(bf16[2,2,256,12,64]{2,4,3,1,0:T(8,128)(2,1)} %get-tuple-element.464, s32[]{:T(128)S(6)} %copy.54, f32[2,12,256,768]{3,2,1,0:T(8,128)} %copy-done.2, f32[2,12,256]{2,1,0:T(8,128)S(1)} %get-tuple-element.433, pred[2,256,768]{2,1,0:T(8,128)(4,1)S(1)} %and_or_fusion.4, ...), kind=kOutput, calls=%fused_computation.17.clone.1 | convolution fusion | flops 623247360 | bytes 22438912 | tf_op jit(solution)/shard_map/while/body/eval_jaxpr/vbta,vabj->vtbj/dot_general | solution.py:132
  196.4 5.4 fusion.151
  201.8 4.6 exponential_reduce_fusion.2
  206.4 1.8 copy-done.2
  208.3 10.4 %fusion.152 = bf16[2,2,256,12,64]{2,4,3,1,0:T(8,128)(2,1)} fusion(bf16[2,2,256,12,64]{2,4,3,1,0:T(8,128)(2,1)} %get-tuple-element.464, s32[]{:T(128)S(6)} %copy.54, f32[2,12,256,768]{3,2,1,0:T(8,128)} %copy-done.2, f32[2,12,256]{2,1,0:T(8,128)S(1)} %get-tuple-element.433, pred[2,256,768]{2,1,0:T(8,128)(4,1)S(1)} %and_or_fusion.4, ...), kind=kOutput, calls=%fused_computation.17.clone.1 | convolution fusion | flops 623247360 | bytes 22438912 | tf_op jit(solution)/shard_map/while/body/eval_jaxpr/vbta,vabj->vtbj/dot_general | solution.py:132
  219.1 4.5 fusion.129
  224.2 11.3 %fusion.95 = (u8[256,3072]{1,0:T(8,128)(4,1)S(1)}, u8[256,3072]{1,0:T(8,128)(4,1)S(1)}, f32[4,256,3072]{2,1,0:T(8,128)S(1)}) fusion(f32[3072]{0:T(1024)S(1)} %copy-done.29, bf16[768,3072]{1,0:T(8,128)(2,1)} %param.33, f32[4,256,768]{2,1,0:T(8,128)S(1)} %get-tuple-element.285, f32[768]{0:T(1024)S(1)} %copy-done.39, f32[768]{0:T(1024)S(1)} %copy-done.36, ...), kind=kOutput, calls=%fused_computation.138 | convolution fusion | flops 4878237696 | bytes 22046720 | tf_op jit(solution)/shard_map/rsd,df->rsf/dot_general | solution.py:148
  235.5 28.7 %fusion.63 = f32[4,256,3072]{2,1,0:T(8,128)} fusion(f32[4,256,3072]{2,1,0:T(8,128)S(1)} %get-tuple-element.286, f32[3072]{0:T(1024)S(1)} %copy-done.29, u8[256,3072]{1,0:T(8,128)(4,1)S(1)} %get-tuple-element.206, u8[256,3072]{1,0:T(8,128)(4,1)S(1)} %get-tuple-element.205), kind=kLoop, calls=%fused_computation.76 | loop fusion | flops 213909504 | bytes 26750976 | tf_op jit(solution)/shard_map/jvp()/erfc | solution.py:149
  264.2 20.7 %multiply_reduce_fusion.6 = (f32[4,256]{1,0:T(4,128)}, f32[4,256]{1,0:T(4,128)}, f32[4,256,768]{2,1,0:T(8,128)}) fusion(f32[768]{0:T(1024)} %param.31, f32[4,256]{1,0:T(4,128)} %copy-done.21, f32[4,256,768]{2,1,0:T(8,128)} %copy-done.6, f32[4,256]{1,0:T(4,128)} %copy-done.16, bf16[768,3072]{1,0:T(8,128)(2,1)} %param.33, f32[4,256,3072]{2,1,0:T(8,128)} %fusion.63, ...), kind=kOutput, calls=%fused_computation.142 | convolution fusion | flops 9717938176 | bytes 42503168 | tf_op jit(solution)/shard_map/rsf,df->rsd/dot_general | solution.py:161
  286.9 7.0 convolution_convert_fusion
  293.8 2.6 copy.39
  296.4 114.5 %while.29 = (s32[]{:T(128)}, bf16[2,2,256,12,64]{2,4,3,1,0:T(8,128)(2,1)}, f32[2,2,768,12,64]{2,4,3,1,0:T(8,128)}, f32[2,2,768,12,64]{2,4,3,1,0:T(8,128)}, bf16[...) while((s32[]{:T(128)}, ...), condition=%wide.region_12.13_spmd.clone, body=%wide.region_10.12_spmd.clone.sunk | while | flops 3093621504 | bytes 260910336 | solution.py:191
  298.6 4.6 fusion.161
  303.2 6.4 copy-done.1
  309.6 7.7 %bitcast_dynamic-update-slice_fusion.11 = f32[2,2,768,12,64]{2,4,3,1,0:T(8,128)} fusion(f32[2,2,768,12,64]{2,4,3,1,0:T(8,128)} %get-tuple-element.502, s32[]{:T(128)S(6)} %copy.64, f32[2,12,256,768]{3,2,1,0:T(8,128)S(1)} %fusion.161, f32[2,12,256]{2,1,0:T(8,128)S(1)} %dynamic-slice_bitcast_fusion.9, pred[2,256,768]{2,1,0:T(8,128)(4,1)S(1)} %and_or_fusion.5, ...), kind=kOutput, calls=%fused_computation.40.clone.1 | convolution fusion | flops 622854144 | bytes 24798208 | tf_op jit(solution)/shard_map/while/body/eval_jaxpr/ghqk,gqhd->gkhd/dot_general | solution.py:172
  317.3 15.0 %multiply_reduce_fusion.8 = (f32[2,12,256]{2,1,0:T(8,128)S(1)}, f32[2,12,256,768]{3,2,1,0:T(8,128)}) fusion(f32[2,12,256,768]{3,2,1,0:T(8,128)} %copy-done.1, f32[2,12,256]{2,1,0:T(8,128)S(1)} %dynamic-slice_bitcast_fusion.9, pred[2,256,768]{2,1,0:T(8,128)(4,1)S(1)} %and_or_fusion.5, bf16[2,2,768,12,64]{2,4,3,1,0:T(8,128)(2,1)} %get-tuple-element.524, ...), kind=kOutput, calls=%fused_computation.32.clone.1 | convolution fusion | flops 627566592 | bytes 41337856 | tf_op jit(solution)/shard_map/while/body/eval_jaxpr/gqhd,gkhd->ghqk/dot_general | solution.py:178
  332.3 13.5 %multiply_convert_fusion.6 = bf16[2,12,256,768]{3,2,1,0:T(8,128)(2,1)S(1)} fusion(f32[2,12,256,768]{3,2,1,0:T(8,128)} %get-tuple-element.450, f32[2,12,256,768]{3,2,1,0:T(8,128)} %copy-done.1, f32[2,12,256]{2,1,0:T(8,128)S(1)} %get-tuple-element.451, f32[2,12,256]{2,1,0:T(8,128)S(1)} %dynamic-slice_bitcast_fusion.9, ...), kind=kLoop, calls=%fused_computation.31.clone.1 | loop fusion | flops 28311552 | bytes 47628288 | tf_op jit(solution)/shard_map/while/body/eval_jaxpr/convert_element_type | solution.py:182
  345.8 3.9 bitcast_dynamic-update-slice_fusion.9
  349.7 3.9 bitcast_dynamic-update-slice_fusion.10
  355.6 4.6 fusion.161
  360.2 6.4 copy-done.1
  366.7 7.7 %bitcast_dynamic-update-slice_fusion.11 = f32[2,2,768,12,64]{2,4,3,1,0:T(8,128)} fusion(f32[2,2,768,12,64]{2,4,3,1,0:T(8,128)} %get-tuple-element.502, s32[]{:T(128)S(6)} %copy.64, f32[2,12,256,768]{3,2,1,0:T(8,128)S(1)} %fusion.161, f32[2,12,256]{2,1,0:T(8,128)S(1)} %dynamic-slice_bitcast_fusion.9, pred[2,256,768]{2,1,0:T(8,128)(4,1)S(1)} %and_or_fusion.5, ...), kind=kOutput, calls=%fused_computation.40.clone.1 | convolution fusion | flops 622854144 | bytes 24798208 | tf_op jit(solution)/shard_map/while/body/eval_jaxpr/ghqk,gqhd->gkhd/dot_general | solution.py:172
  374.3 15.0 %multiply_reduce_fusion.8 = (f32[2,12,256]{2,1,0:T(8,128)S(1)}, f32[2,12,256,768]{3,2,1,0:T(8,128)}) fusion(f32[2,12,256,768]{3,2,1,0:T(8,128)} %copy-done.1, f32[2,12,256]{2,1,0:T(8,128)S(1)} %dynamic-slice_bitcast_fusion.9, pred[2,256,768]{2,1,0:T(8,128)(4,1)S(1)} %and_or_fusion.5, bf16[2,2,768,12,64]{2,4,3,1,0:T(8,128)(2,1)} %get-tuple-element.524, ...), kind=kOutput, calls=%fused_computation.32.clone.1 | convolution fusion | flops 627566592 | bytes 41337856 | tf_op jit(solution)/shard_map/while/body/eval_jaxpr/gqhd,gkhd->ghqk/dot_general | solution.py:178
  389.4 13.5 %multiply_convert_fusion.6 = bf16[2,12,256,768]{3,2,1,0:T(8,128)(2,1)S(1)} fusion(f32[2,12,256,768]{3,2,1,0:T(8,128)} %get-tuple-element.450, f32[2,12,256,768]{3,2,1,0:T(8,128)} %copy-done.1, f32[2,12,256]{2,1,0:T(8,128)S(1)} %get-tuple-element.451, f32[2,12,256]{2,1,0:T(8,128)S(1)} %dynamic-slice_bitcast_fusion.9, ...), kind=kLoop, calls=%fused_computation.31.clone.1 | loop fusion | flops 28311552 | bytes 47628288 | tf_op jit(solution)/shard_map/while/body/eval_jaxpr/convert_element_type | solution.py:182
  402.9 3.8 bitcast_dynamic-update-slice_fusion.9
  406.7 4.0 bitcast_dynamic-update-slice_fusion.10
  410.9 9.6 %copy.42 = f32[4,768,768]{2,1,0:T(8,128)} copy(f32[4,768,768]{1,2,0:T(8,128)} %bitcast.177) | data formatting | bytes 18874368 | tf_op jit(solution)/shard_map/reshape | solution.py:205
  420.5 4.1 convert.21
  424.7 1.9 fusion.125
  427.8 6.2 collective-permute-start.7
  434.0 9.7 %copy.40 = f32[4,768,768]{2,1,0:T(8,128)} copy(f32[4,768,768]{1,2,0:T(8,128)} %bitcast.178) | data formatting | bytes 18874368 | tf_op jit(solution)/shard_map/reshape | solution.py:204
  443.7 4.1 convert.19
  447.8 1.9 fusion.124
  451.0 5.7 collective-permute-start.5
  456.7 2.6 copy.44
  459.3 7.1 %collective-permute-done.6 = bf16[4,256,768]{2,1,0:T(8,128)(2,1)} collective-permute-done((bf16[4,256,768]{2,1,0:T(8,128)(2,1)}, bf16[4,256,768]{2,1,0:T(8,128)(2,1)}, u32[]{:S(2)}, u32[]{:S(2)}) %collective-permute-start.6) | collective-permute-done | bytes 1572896 | tf_op jit(solution)/shard_map/ppermute | solution.py:16
  466.5 67.0 %collective-permute-done.7 = bf16[4,256,768]{2,1,0:T(8,128)(2,1)} collective-permute-done((bf16[4,256,768]{2,1,0:T(8,128)(2,1)}, bf16[4,256,768]{2,1,0:T(8,128)(2,1)}, u32[]{:S(2)}, u32[]{:S(2)}) %collective-permute-start.7) | collective-permute-done | bytes 1572896 | tf_op jit(solution)/shard_map/ppermute | solution.py:16
  533.5 3.3 fusion.90
  536.8 30.2 %collective-permute-done.5 = bf16[4,256,768]{2,1,0:T(8,128)(2,1)} collective-permute-done((bf16[4,256,768]{2,1,0:T(8,128)(2,1)}, bf16[4,256,768]{2,1,0:T(8,128)(2,1)}, u32[]{:S(2)}, u32[]{:S(2)}) %collective-permute-start.5) | collective-permute-done | bytes 1572896 | tf_op jit(solution)/shard_map/ppermute | solution.py:16
  567.1 3.3 fusion.92
  570.5 4.1 multiply_reduce_fusion.5
  574.8 3.3 select_convert_fusion
  578.2 2.0 convolution_bitcast_fusion
  580.2 14.3 %add_convert_fusion.3 = bf16[4,256,768]{2,1,0:T(8,128)(2,1)} fusion(f32[4,256,768]{2,1,0:T(8,128)} %copy-done.6, bf16[3072,768]{1,0:T(8,128)(2,1)} %param.35, f32[4,256,3072]{2,1,0:T(8,128)} %fusion.63, f32[4,256,3072]{2,1,0:T(8,128)} %copy-done.8, f32[3072]{0:T(1024)S(1)} %copy-done.30, f32[768]{0:T(1024)S(1)} %copy-done.40), kind=kOutput, calls=%fused_computation.130 | convolution fusion | flops 4846780416 | bytes 34618368 | tf_op jit(solution)/shard_map/rsf,fd->rsd/dot_general | solution.py:153
  594.5 110.6 %all-reduce.2.cloned.1.call-done = f32[50,768]{1,0:T(8,128)} async-done(((f32[50,768]{1,0:T(8,128)}), f32[50,768]{1,0:T(8,128)}) %all-reduce.2.cloned.1.call-update) | async-done | bytes 153616 | tf_op jit(solution)/shard_map/psum | solution.py:226
  (160 shorter events, 24.0 us)
Async XLA Ops:
  7.2 6.3 copy-start
  7.2 6.3 copy-start.34
  7.2 697.9 %all-reduce.2.cloned.1.call-start = ((), (), s32[]{:S(2)}) async-start(), calls=%async_computation | async-start | bytes 344064 | tf_op jit(solution)/shard_map/psum | solution.py:226
  8.1 5.4 copy-start.38
  9.6 3.3 copy-start.32
  12.9 5.0 copy-start.4
  12.9 4.9 copy-start.14
  13.5 4.4 copy-start.19
  20.2 40.4 %collective-permute-start.3 = (bf16[4,256,768]{2,1,0:T(8,128)(2,1)}, bf16[4,256,768]{2,1,0:T(8,128)(2,1)}, u32[]{:S(2)}, u32[]{:S(2)}) collective-permute-start(bf16[4,256,768]{2,1,0:T(8,128)(2,1)} %get-tuple-element.275), channel_id=1, source_target_pairs={{1,0},{2,1},{3,2},{4,3},{5,4},{6,5},{7,6},{9,8},{10,9},{11,10},{12... | collective-permute-start | bytes 4718600 | tf_op jit(solution)/shard_map/ppermute | solution.py:16
  21.5 106.0 %collective-permute-start.2 = (bf16[4,256,768]{2,1,0:T(8,128)(2,1)}, bf16[4,256,768]{2,1,0:T(8,128)(2,1)}, u32[]{:S(2)}, u32[]{:S(2)}) collective-permute-start(bf16[4,256,768]{2,1,0:T(8,128)(2,1)} %get-tuple-element.275), channel_id=1, source_target_pairs={{0,1},{1,2},{2,3},{3,4},{4,5},{5,6},{6,7},{8,9},{9,10},{10,11},{11... | collective-permute-start | bytes 4718600 | tf_op jit(solution)/shard_map/ppermute | solution.py:16
  28.2 109.8 %collective-permute-start.1 = (bf16[4,256,768]{2,1,0:T(8,128)(2,1)}, bf16[4,256,768]{2,1,0:T(8,128)(2,1)}, u32[]{:S(2)}, u32[]{:S(2)}) collective-permute-start(bf16[4,256,768]{2,1,0:T(8,128)(2,1)} %get-tuple-element.277), channel_id=1, source_target_pairs={{1,0},{2,1},{3,2},{4,3},{5,4},{6,5},{7,6},{9,8},{10,9},{11,10},{12... | collective-permute-start | bytes 4718600 | tf_op jit(solution)/shard_map/ppermute | solution.py:16
  29.5 131.6 %collective-permute-start = (bf16[4,256,768]{2,1,0:T(8,128)(2,1)}, bf16[4,256,768]{2,1,0:T(8,128)(2,1)}, u32[]{:S(2)}, u32[]{:S(2)}) collective-permute-start(bf16[4,256,768]{2,1,0:T(8,128)(2,1)} %get-tuple-element.277), channel_id=1, source_target_pairs={{0,1},{1,2},{2,3},{3,4},{4,5},{5,6},{6,7},{8,9},{9,10},{10,11},{11... | collective-permute-start | bytes 4718600 | tf_op jit(solution)/shard_map/ppermute | solution.py:16
  38.1 4.1 copy-start.31
  38.1 0.6 copy-start.28
  178.2 6.4 copy-start.2
  178.2 6.4 copy-start.12
  184.7 10.4 %copy-start.13 = (f32[2,2,12,256]{3,2,1,0:T(8,128)}, f32[2,2,12,256]{3,2,1,0:T(8,128)S(1)}, u32[]{:S(2)}) copy-start(f32[2,2,12,256]{3,2,1,0:T(8,128)S(1)} %get-tuple-element.476) | copy-start | bytes 147460 | tf_op jit(solution)/shard_map/while
  201.8 6.4 copy-start.2
  201.8 6.4 copy-start.12
  208.2 10.4 %copy-start.13 = (f32[2,2,12,256]{3,2,1,0:T(8,128)}, f32[2,2,12,256]{3,2,1,0:T(8,128)S(1)}, u32[]{:S(2)}) copy-start(f32[2,2,12,256]{3,2,1,0:T(8,128)S(1)} %get-tuple-element.476) | copy-start | bytes 147460 | tf_op jit(solution)/shard_map/while
  219.1 5.0 copy-start.29
  219.1 5.0 copy-start.36
  219.1 5.0 copy-start.39
  223.6 11.9 %copy-start.6 = (f32[4,256,768]{2,1,0:T(8,128)}, f32[4,256,768]{2,1,0:T(8,128)S(1)}, u32[]{:S(2)}) copy-start(f32[4,256,768]{2,1,0:T(8,128)S(1)} %get-tuple-element.285) | copy-start | bytes 9437188
  223.6 11.9 %copy-start.16 = (f32[4,256]{1,0:T(4,128)}, f32[4,256]{1,0:T(4,128)S(1)}, u32[]{:S(2)}) copy-start(f32[4,256]{1,0:T(4,128)S(1)} %broadcast_multiply_fusion.4) | copy-start | bytes 12292
  224.1 11.4 %copy-start.21 = (f32[4,256]{1,0:T(4,128)}, f32[4,256]{1,0:T(4,128)S(1)}, u32[]{:S(2)}) copy-start(f32[4,256]{1,0:T(4,128)S(1)} %add_rsqrt_fusion) | copy-start | bytes 12292
  235.5 28.7 %copy-start.8 = (f32[4,256,3072]{2,1,0:T(8,128)}, f32[4,256,3072]{2,1,0:T(8,128)S(1)}, u32[]{:S(2)}) copy-start(f32[4,256,3072]{2,1,0:T(8,128)S(1)} %get-tuple-element.286) | copy-start | bytes 37748740
  285.6 0.7 copy-start.23
  286.3 0.6 copy-start.25
  303.1 6.4 copy-start.1
  317.3 28.5 %slice-start = ((s8[4718592]{0:T(1024)(128)(4,1)}), s8[524288]{0:T(1024)(128)(4,1)S(1)}, s32[]{:S(2)}) async-start(s8[4718592]{0:T(1024)(128)(4,1)} %bitcast.172), calls=%async_computation.1 | async-start | bytes 1048576 | tf_op jit(solution)/shard_map/while
  332.3 13.5 %slice-start.1 = ((s8[4718592]{0:T(1024)(128)(4,1)}), s8[4194304]{0:T(1024)(128)(4,1)S(1)}, s32[]{:S(2)}) async-start(s8[4718592]{0:T(1024)(128)(4,1)} %bitcast.172), calls=%async_computation.2 | async-start | bytes 8388608 | tf_op jit(solution)/shard_map/while
  345.8 3.9 copy-start.3
  360.2 6.4 copy-start.1
  374.3 28.5 %slice-start = ((s8[4718592]{0:T(1024)(128)(4,1)}), s8[524288]{0:T(1024)(128)(4,1)S(1)}, s32[]{:S(2)}) async-start(s8[4718592]{0:T(1024)(128)(4,1)} %bitcast.172), calls=%async_computation.1 | async-start | bytes 1048576 | tf_op jit(solution)/shard_map/while
  389.4 13.5 %slice-start.1 = ((s8[4718592]{0:T(1024)(128)(4,1)}), s8[4194304]{0:T(1024)(128)(4,1)S(1)}, s32[]{:S(2)}) async-start(s8[4718592]{0:T(1024)(128)(4,1)} %bitcast.172), calls=%async_computation.2 | async-start | bytes 8388608 | tf_op jit(solution)/shard_map/while
  402.9 3.8 copy-start.3
  426.5 39.9 %collective-permute-start.6 = (bf16[4,256,768]{2,1,0:T(8,128)(2,1)}, bf16[4,256,768]{2,1,0:T(8,128)(2,1)}, u32[]{:S(2)}, u32[]{:S(2)}) collective-permute-start(bf16[4,256,768]{2,1,0:T(8,128)(2,1)} %get-tuple-element.273), channel_id=1, source_target_pairs={{1,0},{2,1},{3,2},{4,3},{5,4},{6,5},{7,6},{9,8},{10,9},{11,10},{12... | collective-permute-start | bytes 4718600 | tf_op jit(solution)/shard_map/ppermute | solution.py:16
  427.8 105.6 %collective-permute-start.7 = (bf16[4,256,768]{2,1,0:T(8,128)(2,1)}, bf16[4,256,768]{2,1,0:T(8,128)(2,1)}, u32[]{:S(2)}, u32[]{:S(2)}) collective-permute-start(bf16[4,256,768]{2,1,0:T(8,128)(2,1)} %get-tuple-element.274), channel_id=1, source_target_pairs={{0,1},{1,2},{2,3},{3,4},{4,5},{5,6},{6,7},{8,9},{9,10},{10,11},{11... | collective-permute-start | bytes 4718600 | tf_op jit(solution)/shard_map/ppermute | solution.py:16
  449.7 87.1 %collective-permute-start.4 = (bf16[4,256,768]{2,1,0:T(8,128)(2,1)}, bf16[4,256,768]{2,1,0:T(8,128)(2,1)}, u32[]{:S(2)}, u32[]{:S(2)}) collective-permute-start(bf16[4,256,768]{2,1,0:T(8,128)(2,1)} %get-tuple-element.271), channel_id=1, source_target_pairs={{1,0},{2,1},{3,2},{4,3},{5,4},{6,5},{7,6},{9,8},{10,9},{11,10},{12... | collective-permute-start | bytes 4718600 | tf_op jit(solution)/shard_map/ppermute | solution.py:16
  451.0 116.1 %collective-permute-start.5 = (bf16[4,256,768]{2,1,0:T(8,128)(2,1)}, bf16[4,256,768]{2,1,0:T(8,128)(2,1)}, u32[]{:S(2)}, u32[]{:S(2)}) collective-permute-start(bf16[4,256,768]{2,1,0:T(8,128)(2,1)} %get-tuple-element.272), channel_id=1, source_target_pairs={{0,1},{1,2},{2,3},{3,4},{4,5},{5,6},{6,7},{8,9},{9,10},{10,11},{11... | collective-permute-start | bytes 4718600 | tf_op jit(solution)/shard_map/ppermute | solution.py:16
  536.8 33.6 %copy-start.5 = (f32[4,256,768]{2,1,0:T(8,128)S(1)}, f32[4,256,768]{2,1,0:T(8,128)}, u32[]{:S(2)}) copy-start(f32[4,256,768]{2,1,0:T(8,128)} %copy-done.4) | copy-start | bytes 9437188
  536.8 33.6 %copy-start.11 = (bf16[4,256,768]{2,1,0:T(8,128)(2,1)S(1)}, bf16[4,256,768]{2,1,0:T(8,128)(2,1)}, u32[]{:S(2)}) copy-start(bf16[4,256,768]{2,1,0:T(8,128)(2,1)} %copy.44) | copy-start | bytes 4718596
  536.8 33.6 %copy-start.15 = (f32[4,256]{1,0:T(4,128)S(1)}, f32[4,256]{1,0:T(4,128)}, u32[]{:S(2)}) copy-start(f32[4,256]{1,0:T(4,128)} %copy-done.14) | copy-start | bytes 12292
  536.8 33.6 %copy-start.20 = (f32[4,256]{1,0:T(4,128)S(1)}, f32[4,256]{1,0:T(4,128)}, u32[]{:S(2)}) copy-start(f32[4,256]{1,0:T(4,128)} %copy-done.19) | copy-start | bytes 12292
  536.8 33.6 %copy-start.35 = (f32[768]{0:T(1024)S(1)}, f32[768]{0:T(1024)}, u32[]{:S(2)}) copy-start(f32[768]{0:T(1024)} %param.25) | copy-start | bytes 9220
  570.4 4.3 copy-start.7
  570.5 4.3 copy-start.9
  570.5 4.3 copy-start.10
  570.5 4.3 copy-start.17
  570.5 4.3 copy-start.22
  570.5 4.3 copy-start.24
  570.5 4.3 copy-start.26
  570.5 4.3 copy-start.27
  570.5 4.3 copy-start.33
  570.5 4.3 copy-start.37
  574.8 3.4 copy-start.18
  574.8 5.4 copy-start.30
  574.8 5.4 copy-start.40
Sparse Core Ops, SparseCore 0:
  580.3 124.7 all-reduce.1
where the time goes:
time: 721 us; the launch traced here: 714 us
  waiting for transfers between devices  317 us (44%)
  matrix products  173 us (24%)
  other arithmetic  102 us (14%)
  local copies, waits for them, and re-layouts  76.2 us (11%)
  starting transfers between devices  29.7 us (4%)
  between operations  14.9 us (2%)
    ppermute x8, waiting for transfers between devices, passed_along(): return lax.ppermute(block, axis, route)  206 us
    psum x1, waiting for transfers between devices, body(): prompt_gradient = lax.psum(prompt_part, ('batch', 'seq'))  111 us
    dot_general x2, matrix products, backward_block(): jnp.einsum('gqhd,gkhd->ghqk', grad_blk, value_blk, preferred_element_type...  30 us
    ppermute x8, starting transfers between devices, passed_along(): return lax.ppermute(block, axis, route)  29.6 us
    another operation x1, other arithmetic, body(): jax.nn.gelu(inner, approximate=False)  28.7 us
    convert_element_type x2, other arithmetic, backward_block(): score_grad = (attention_weights * (prob_grad - inner)).astype(jnp.bfloat16)  27 us
    dot_general x2, matrix products, forward_block(): jnp.einsum('vbta,vabj->vtbj', attention_weights, value_blk, preferred_ele...  20.8 us
    dot_general x1, matrix products, body(): jnp.einsum('rsf,df->rsd', upper_grad, w_up, preferred_element_type=jnp.fl...  20.7 us
  transfers between devices with their start and end apart: 9, of which 7 were waited for; matrix products, arithmetic and copies ran while one was open for 8% of the time, Pallas kernels for 0%

commit v1 on v0

--- a/solution.py
+++ b/solution.py
@@ -1,6 +1,10 @@
+import functools
+
 import jax
 import jax.numpy as jnp
 from jax import lax
+from jax.experimental import pallas as pl
+from jax.experimental.pallas import tpu as pltpu
 from jax.sharding import PartitionSpec as P
 
 ATTENTION_HEADS = 12
@@ -50,7 +54,7 @@
     return jnp.where(permitted_mask[:, None], scores, -1e30)
 
 
-def body(
+def general_body(
     tokens,
     prompts,
     image_id,
@@ -227,6 +231,303 @@
     return (output, token_gradient, prompt_gradient)
 
 
+HALO = 64
+SLOTS = 320
+KEYS = 256
+PAIR = 2 * HEAD_FEATURES
+SCALE = HEAD_FEATURES ** (-0.5)
+ERFC_RATE = 0.39
+ERFC_TERMS = (
+    0.23532515356929604,
+    0.09138882070894727,
+    0.6495583974454544,
+    -0.6353990518468564,
+    0.8866636223583176,
+    -0.22753694392981927,
+)
+
+
+def dot(a, b):
+    return lax.dot_general(a, b, (((1,), (0,)), ((), ())), preferred_element_type=jnp.float32)
+
+
+def dot_nt(a, b):
+    return lax.dot_general(a, b, (((1,), (1,)), ((), ())), preferred_element_type=jnp.float32)
+
+
+def dot_tn(a, b):
+    return lax.dot_general(a, b, (((0,), (0,)), ((), ())), preferred_element_type=jnp.float32)
+
+
+def gelu_parts(upper):
+    size = jnp.abs(upper)
+    t = 1.0 / (1.0 + (ERFC_RATE * 0.5**0.5) * size)
+    tail = jnp.full_like(t, 0.5 * ERFC_TERMS[-1])
+    for term in ERFC_TERMS[-2::-1]:
+        tail = tail * t + 0.5 * term
+    bell = jnp.exp(-0.5 * upper * upper)
+    tail = tail * t * bell
+    below = jnp.where(upper < 0, tail, 1.0 - tail)
+    return upper * below, below + upper * (bell * 0.3989422804014327)
+
+
+def slot_map(ids, index, span):
+    lane = lax.broadcasted_iota(jnp.int32, ids.shape, 1)
+
+    def first(image):
+        return jnp.min(jnp.where(ids == image, lane, ids.shape[1] * 2), axis=1, keepdims=True)
+
+    low = index * span
+    start = first(index)
+    end = start + IMAGE_TOKENS
+    before = jnp.where(index == 0, low, jnp.maximum(first(index - 1) + IMAGE_TOKENS, low))
+    after = jnp.where(
+        index == IMAGES_PER_ROW - 1, low + span, jnp.minimum(first(index + 1), low + span)
+    )
+    spot = lax.broadcasted_iota(jnp.int32, (1, span + 2 * HALO), 1)
+    place = low + jnp.where(
+        spot < span, spot, jnp.where(spot < span + HALO, spot - span - HALO, spot - HALO)
+    )
+    lead = jnp.maximum(start - before, 0)
+    slot = jnp.where((place >= end) & (place < after), IMAGE_TOKENS + lead + place - end, -1)
+    slot = jnp.where((place >= before) & (place < start), IMAGE_TOKENS + place - before, slot)
+    return jnp.where((place >= start) & (place < end), place - start, slot)
+
+
+def row_kernel(
+    ids, tok, tok_halo, cot, cot_halo, prom, g1, b1, w_qkv, b_qv, w_out, b_out, g2, b2, w_up, b_up, w_down, b_down,
+    out, out_halo, tgr, tgr_halo, pgr,
+    pick, ins, n1, inv1, wide, qkv, probs, turned, hid, n2, inv2, act, upg, og, grad,
+):
+    index = lax.axis_index("seq")
+    span, width = tok.shape[1], tok.shape[2]
+    ff = w_up.shape[1]
+    bf = jnp.bfloat16
+    slot = slot_map(ids[0], index, span)
+    slots = lax.broadcasted_iota(jnp.int32, (SLOTS, span + 2 * HALO), 0)
+    pick[...] = jnp.where(slots == slot, 1.0, 0.0).astype(bf)
+
+    first_rows = lax.broadcasted_iota(jnp.int32, (64, 1), 0)
+    is_prompt = (first_rows >= 1) & (first_rows <= PROMPTS)
+    for r in range(0, SLOTS, 64):
+        x = dot(pick[r : r + 64, :span], tok[0]) + dot(pick[r : r + 64, span:], tok_halo[0])
+        if r == 0:
+            x = jnp.where(is_prompt, prom[...], x)
+        ins[r : r + 64] = x
+        mean = jnp.mean(x, axis=-1, keepdims=True)
+        c = x - mean
+        inv = lax.rsqrt(jnp.mean(c * c, axis=-1, keepdims=True) + 1e-06)
+        c = c * inv
+        if r < KEYS:
+            n1[r : r + 64] = c
+            inv1[r : r + 64] = inv
+        wide[r : r + 64] = (c * g1[...] + b1[...]).astype(bf)
+
+    for c in range(0, width, 256):
+        q = dot(wide[:KEYS], w_qkv[:, c : c + 256]) + b_qv[:, c : c + 256]
+        qkv[:KEYS, c : c + 256] = (q * SCALE).astype(bf)
+        k = dot(wide[:KEYS], w_qkv[:, width + c : width + c + 256])
+        qkv[:KEYS, width + c : width + c + 256] = k.astype(bf)
+        v = dot(wide[...], w_qkv[:, 2 * width + c : 2 * width + c + 256]) + b_qv[:, width + c : width + c + 256]
+        qkv[:, 2 * width + c : 2 * width + c + 256] = v.astype(bf)
+
+    lane = lax.broadcasted_iota(jnp.int32, (1, PAIR), 1)
+    low_half = jnp.where(lane < HEAD_FEATURES, 1.0, 0.0).astype(bf)
+    high_half = jnp.where(lane < HEAD_FEATURES, 0.0, 1.0).astype(bf)
+
+    def both(x):
+        return jnp.concatenate([x * low_half, x * high_half], axis=0)
+
+    def own_halves(x):
+        return x[:HEAD_FEATURES, :KEYS], x[HEAD_FEATURES:, KEYS:]
+
+    tail_rows = lax.broadcasted_iota(jnp.int32, (16, 1), 0) + (KEYS - 16)
+    for p in range(width // PAIR):
+        at = p * PAIR
+        qp = qkv[:KEYS, at : at + PAIR]
+        kp = qkv[:KEYS, width + at : width + at + PAIR]
+        vp = qkv[:KEYS, 2 * width + at : 2 * width + at + PAIR]
+        st = dot_nt(kp, both(qp))
+        upper, lower = st[: KEYS - 16], st[KEYS - 16 :]
+        lower = jnp.where(tail_rows < IMAGE_TOKENS, lower, -1e30)
+        top = jnp.maximum(jnp.max(upper, axis=0, keepdims=True), jnp.max(lower, axis=0, keepdims=True))
+        upper = jnp.exp(upper - top)
+        lower = jnp.exp(lower - top)
+        total = jnp.sum(upper, axis=0, keepdims=True) + jnp.sum(lower, axis=0, keepdims=True)
+        share = 1.0 / total
+        probs[p, : KEYS - 16] = (upper * share).astype(bf)
+        probs[p, KEYS - 16 :] = (lower * share).astype(bf)
+        head0, head1 = own_halves(dot_tn(vp, probs[p]))
+        turned[at : at + HEAD_FEATURES] = head0.astype(bf)
+        turned[at + HEAD_FEATURES : at + PAIR] = head1.astype(bf)
+
+    key_rows = lax.broadcasted_iota(jnp.int32, (KEYS, 1), 0)
+    attended = turned[...].T
+    wide[:KEYS] = jnp.where(key_rows < IMAGE_TOKENS, attended, qkv[:KEYS, 2 * width :])
+    wide[KEYS:] = qkv[KEYS:, 2 * width :]
+    for c in range(0, width, 256):
+        hid[:, c : c + 256] = ins[:, c : c + 256] + dot(wide[...], w_out[:, c : c + 256]) + b_out[:, c : c + 256]
+
+    for r in range(0, SLOTS, 64):
+        x = hid[r : r + 64]
+        mean = jnp.mean(x, axis=-1, keepdims=True)
+        c = x - mean
+        inv = lax.rsqrt(jnp.mean(c * c, axis=-1, keepdims=True) + 1e-06)
+        c = c * inv
+        if r < KEYS:
+            n2[r : r + 64] = c
+            inv2[r : r + 64] = inv
+        wide[r : r + 64] = (c * g2[...] + b2[...]).astype(bf)
+    for r in range(0, KEYS, 64):
+        x = dot(pick[r : r + 64, :span], cot[0]) + dot(pick[r : r + 64, span:], cot_halo[0])
+        if r + 64 == KEYS:
+            x = jnp.where(first_rows < IMAGE_TOKENS - r, x, 0.0)
+        og[r : r + 64] = x.astype(bf)
+
+    for c in range(0, ff, 256):
+        upper = dot(wide[...], w_up[:, c : c + 256]) + b_up[:, c : c + 256]
+        act_grad = dot_nt(og[...], w_down[c : c + 256, :])
+        value, slope = gelu_parts(upper)
+        act[:, c : c + 256] = value.astype(bf)
+        upg[:, c : c + 256] = (act_grad * slope[:KEYS]).astype(bf)
+    for c in range(0, width, 256):
+        y = hid[:, c : c + 256] + dot(act[...], w_down[:, c : c + 256]) + b_down[:, c : c + 256]
+        wide[:, c : c + 256] = y.astype(bf)
+        grad[:, c : c + 256] = dot_nt(upg[...], w_up[c : c + 256, :])
+    out[0] = dot_tn(pick[:, :span], wide[...]).astype(bf)
+    out_halo[0] = dot_tn(pick[:, span:], wide[...]).astype(bf)
+
+    for r in range(0, KEYS, 64):
+        e = grad[r : r + 64] * g2[...]
+        n = n2[r : r + 64]
+        mean = jnp.mean(e, axis=-1, keepdims=True)
+        part = jnp.mean(e * n, axis=-1, keepdims=True)
+        h = og[r : r + 64].astype(jnp.float32) + inv2[r : r + 64] * (e - mean - n * part)
+        hid[r : r + 64] = h
+        wide[r : r + 64] = h.astype(bf)
+    for c in range(0, width, 256):
+        og[:, c : c + 256] = dot_nt(wide[:KEYS], w_out[c : c + 256, :]).astype(bf)
+
+    for p in range(width // PAIR):
+        at = p * PAIR
+        qp = qkv[:KEYS, at : at + PAIR]
+        kp = qkv[:KEYS, width + at : width + at + PAIR]
+        vp = qkv[:KEYS, 2 * width + at : 2 * width + at + PAIR]
+        two_grads = both(og[:, at : at + PAIR])
+        dp = dot_nt(vp, two_grads)
+        pt = probs[p]
+        pf = pt.astype(jnp.float32)
+        inner = jnp.sum(pf * dp, axis=0, keepdims=True)
+        ds = (pf * (dp - inner)).astype(bf)
+        qkv[:KEYS, 2 * width + at : 2 * width + at + PAIR] = dot(pt, two_grads).astype(bf)
+        head0, head1 = own_halves(dot_tn(kp, ds))
+        qkv[:KEYS, width + at : width + at + PAIR] = dot(ds, both(qp)).astype(bf)
+        turned[at : at + HEAD_FEATURES] = (head0 * SCALE).astype(bf)
+        turned[at + HEAD_FEATURES : at + PAIR] = (head1 * SCALE).astype(bf)
+    qkv[:KEYS, :width] = turned[...].T
+
+    for c in range(0, width, 256):
+        grad[:, c : c + 256] = dot_nt(qkv[:KEYS], w_qkv[c : c + 256, :])
+    for r in range(0, KEYS, 64):
+        e = grad[r : r + 64] * g1[...]
+        n = n1[r : r + 64]
+        mean = jnp.mean(e, axis=-1, keepdims=True)
+        part = jnp.mean(e * n, axis=-1, keepdims=True)
+        x = hid[r : r + 64] + inv1[r : r + 64] * (e - mean - n * part)
+        if r == 0:
+            @pl.when(pl.program_id(0) == 0)
+            def _():
+                pgr[...] = x
+
+            @pl.when(pl.program_id(0) > 0)
+            def _():
+                pgr[...] += x
+            x = jnp.where(is_prompt, 0.0, x)
+        wide[r : r + 64] = x.astype(bf)
+    tgr[0] = dot_tn(pick[:KEYS, :span], wide[:KEYS]).astype(bf)
+    tgr_halo[0] = dot_tn(pick[:KEYS, span:], wide[:KEYS]).astype(bf)
+
+
+def swapped(to_left, to_right):
+    count = lax.axis_size("seq")
+    from_right = lax.ppermute(to_left, "seq", [(i, i - 1) for i in range(1, count)])
+    from_left = lax.ppermute(to_right, "seq", [(i, i + 1) for i in range(count - 1)])
+    return from_left, from_right
+
+
+def image_body(
+    tokens, prompts, image_id, prompt_slot, ln1_gain, ln1_bias, w_qkv, bias_qv, w_out, bias_out,
+    ln2_gain, ln2_bias, w_up, bias_up, w_down, bias_down, cotangent,
+):
+    rows, span, width = tokens.shape
+    length = image_id.shape[1]
+    ff = w_up.shape[1]
+    f32, bf = jnp.float32, jnp.bfloat16
+
+    def halo(x):
+        return jnp.concatenate(swapped(x[:, :HALO], x[:, span - HALO :]), axis=1)
+
+    prom = jnp.zeros((64, width), f32).at[1 : PROMPTS + 1].set(prompts)
+
+    def per_row(*shape):
+        return pl.BlockSpec((1,) + shape, lambda r: (r, 0, 0))
+
+    def whole(*shape):
+        return pl.BlockSpec(shape, lambda r: (0,) * len(shape), pipeline_mode=pl.Buffered(1))
+
+    def line(x):
+        return x.reshape(1, -1)
+
+    out, out_halo, tgr, tgr_halo, pgr = pl.pallas_call(
+        row_kernel,
+        grid=(rows,),
+        in_specs=[
+            per_row(1, length), per_row(span, width), per_row(2 * HALO, width), per_row(span, width),
+            per_row(2 * HALO, width), whole(64, width), whole(1, width), whole(1, width), whole(width, 3 * width),
+            whole(1, 2 * width), whole(width, width), whole(1, width), whole(1, width), whole(1, width),
+            whole(width, ff), whole(1, ff), whole(ff, width), whole(1, width),
+        ],
+        out_specs=[
+            per_row(span, width), per_row(2 * HALO, width), per_row(span, width), per_row(2 * HALO, width),
+            pl.BlockSpec((64, width), lambda r: (0, 0)),
+        ],
+        out_shape=[
+            jax.ShapeDtypeStruct((rows, span, width), bf), jax.ShapeDtypeStruct((rows, 2 * HALO, width), bf),
+            jax.ShapeDtypeStruct((rows, span, width), bf), jax.ShapeDtypeStruct((rows, 2 * HALO, width), bf),
+            jax.ShapeDtypeStruct((64, width), f32),
+        ],
+        scratch_shapes=[
+            pltpu.VMEM((SLOTS, span + 2 * HALO), bf), pltpu.VMEM((SLOTS, width), f32), pltpu.VMEM((KEYS, width), f32),
+            pltpu.VMEM((KEYS, 1), f32), pltpu.VMEM((SLOTS, width), bf), pltpu.VMEM((SLOTS, 3 * width), bf),
+            pltpu.VMEM((width // PAIR, KEYS, 2 * KEYS), bf), pltpu.VMEM((width, KEYS), bf),
+            pltpu.VMEM((SLOTS, width), f32), pltpu.VMEM((KEYS, width), f32), pltpu.VMEM((KEYS, 1), f32),
+            pltpu.VMEM((SLOTS, ff), bf), pltpu.VMEM((KEYS, ff), bf), pltpu.VMEM((KEYS, width), bf),
+            pltpu.VMEM((KEYS, width), f32),
+        ],
+        compiler_params=pltpu.CompilerParams(vmem_limit_bytes=60 << 20, dimension_semantics=("arbitrary",)),
+        name="layer_rows",
+    )(
+        image_id[:, None], tokens, halo(tokens), cotangent, halo(cotangent), prom, line(ln1_gain), line(ln1_bias),
+        w_qkv, line(bias_qv), w_out, line(bias_out), line(ln2_gain), line(ln2_bias), w_up, line(bias_up), w_down,
+        line(bias_down),
+    )
+
+    def home(own, sides):
+        from_left, from_right = swapped(sides[:, :HALO], sides[:, HALO:])
+        return own + jnp.concatenate(
+            [from_left, jnp.zeros((rows, span - 2 * HALO, width), bf), from_right], axis=1
+        )
+
+    prompt_gradient = lax.psum(pgr[1 : PROMPTS + 1], ("batch", "seq"))
+    return home(out, out_halo), home(tgr, tgr_halo), prompt_gradient
+
+
+def body(tokens, prompts, image_id, *rest):
+    if lax.axis_size("seq") == IMAGES_PER_ROW and tokens.shape[1] == KEYS:
+        return image_body(tokens, prompts, image_id, *rest)
+    return general_body(tokens, prompts, image_id, *rest)
+
+
 def solution(mesh):
     in_specs = (
         P("batch", "seq", None),

time: 721 us -> 279 us (0.39)
  waiting for transfers between devices: 317 us -> 143 us
  matrix products: 173 us -> 0 us
  other arithmetic: 102 us -> 5.82 us
  Pallas kernels: 0 us -> 76.5 us
  local copies, waits for them, and re-layouts: 76.2 us -> 13.5 us
    dot_general x23 -> x0, matrix products: 173 us -> none  [the longest x2 30 us: backward_block(): jnp.einsum('gqhd,gkhd->ghqk', grad_blk, value_blk, preferred_element_type...]
    ppermute x8, waiting for transfers between devices: 206 us -> 42.3 us  [the longest x4 42.3 us: swapped(): lax.ppermute(to_right, 'seq', [(i, i + 1) for i in range(count - 1)])]
    pallas_call x0 -> x1, Pallas kernels: none -> 76.5 us  [image_body(): pl.pallas_call(row_kernel, grid=(rows,), in_specs=[per_row(1, length), pe...]
    another operation x7 -> x0, other arithmetic: 43.6 us -> none  [the longest x1 28.7 us: body(): jax.nn.gelu(inner, approximate=False)]
    convert_element_type x4 -> x0, other arithmetic: 31.8 us -> none  [the longest x2 27 us: backward_block(): score_grad = (attention_weights * (prob_grad - inner)).astype(jnp.bfloat16)]
    reshape x4 -> x7, local copies, waits for them, and re-layouts: 22.5 us -> 4.15 us  [line(): return x.reshape(1, -1)]
    while x28 -> x0, local copies, waits for them, and re-layouts: 16.6 us -> none
    concatenate x2 -> x1, local copies, waits for them, and re-layouts: 13.2 us -> 0.08 us  [home(): jnp.concatenate([from_left, jnp.zeros((rows, span - 2 * HALO, width), bf)...]
  transfers between devices with their start and end apart: 9 -> 9, of which waited for: 7 -> 5; matrix products, arithmetic and copies ran while one was open for 8% -> 5% of each run, Pallas kernels for 0% -> 0%
where the time goes in v1:
time: 279 us; the launch traced here: 277 us
  waiting for transfers between devices  143 us (51%)
  Pallas kernels  76.5 us (27%)
  starting transfers between devices  24.7 us (9%)
  between operations  14.2 us (5%)
  local copies, waits for them, and re-layouts  13.5 us (5%)
  other arithmetic  5.82 us (2%)
    psum x1, waiting for transfers between devices, image_body(): prompt_gradient = lax.psum(pgr[1:PROMPTS + 1], ('batch', 'seq'))  100 us
    pallas_call x1, Pallas kernels, image_body(): pl.pallas_call(row_kernel, grid=(rows,), in_specs=[per_row(1, length), pe...  76.5 us
    ppermute x4, waiting for transfers between devices, swapped(): lax.ppermute(to_right, 'seq', [(i, i + 1) for i in range(count - 1)])  42.3 us
    ppermute x4, starting transfers between devices, swapped(): lax.ppermute(to_right, 'seq', [(i, i + 1) for i in range(count - 1)])  19.6 us
  transfers between devices with their start and end apart: 9, of which 5 were waited for; matrix products, arithmetic and copies ran while one was open for 5% of the time, Pallas kernels for 0%

profile of v1, /device:TPU:0, one launch (start us, length us, event | category | flops | bytes accessed | tf_op | source)
XLA Modules:
  0.0 277.4 jit_solution(11036187974688836356)
XLA Ops:
  7.2 0.0 copy-start
  7.2 0.0 copy-start.7
  7.2 0.0 copy-start.8
  7.2 0.0 copy-start.9
  7.2 0.0 copy-start.10
  7.2 0.0 copy-start.11
  7.2 0.0 copy-start.12
  7.2 0.0 copy-start.6
  7.2 0.0 copy-start.5
  7.3 0.0 copy-start.3
  7.3 0.0 all-reduce.3.cloned.1.call-start
  7.3 1.3 fusion.1
  8.6 4.9 %collective-permute-start = (bf16[4,64,768]{2,1,0:T(8,128)(2,1)S(1)}, bf16[4,64,768]{2,1,0:T(8,128)(2,1)S(1)}, u32[]{:S(2)}, u32[]{:S(2)}) collective-permute-start(bf16[4,64,768]{2,1,0:T(8,128)(2,1)S(1)} %get-tuple-element.27), channel_id=1, source_target_pairs={{0,1},{1,2},{2,3},{3,4},{4,5},{5,6},{6,7},{8,9},{9,10},{10,11},{11... | collective-permute-start | bytes 1179656 | tf_op jit(solution)/shard_map/ppermute | solution.py:454
  13.5 1.3 collective-permute-start.1
  14.8 0.0 copy-done
  14.8 0.1 fusion
  14.9 4.6 %collective-permute-start.2 = (bf16[4,64,768]{2,1,0:T(8,128)(2,1)S(1)}, bf16[4,64,768]{2,1,0:T(8,128)(2,1)S(1)}, u32[]{:S(2)}, u32[]{:S(2)}) collective-permute-start(bf16[4,64,768]{2,1,0:T(8,128)(2,1)S(1)} %get-tuple-element.25), channel_id=1, source_target_pairs={{0,1},{1,2},{2,3},{3,4},{4,5},{5,6},{6,7},{8,9},{9,10},{10,11},{11... | collective-permute-start | bytes 1179656 | tf_op jit(solution)/shard_map/ppermute | solution.py:454
  19.5 1.3 collective-permute-start.3
  20.8 0.0 copy-done.7
  20.8 0.6 reshape.56.g1
  21.4 0.0 copy-done.8
  21.4 0.6 reshape.57.b1
  22.0 0.0 copy-done.9
  22.0 0.6 reshape.59.b_out
  22.6 0.0 copy-done.10
  22.6 0.6 reshape.60.g2
  23.2 0.0 copy-done.11
  23.2 0.6 reshape.61.b2
  23.8 0.0 copy-done.12
  23.8 0.6 reshape.63.b_down
  24.4 0.0 copy-done.6
  24.4 0.6 reshape.58.b_qv
  25.0 0.0 copy-done.5
  25.0 0.6 broadcast_in_dim.4.ids
  25.6 0.0 copy-done.3
  25.6 0.7 scatter.4.prom
  26.3 13.6 %collective-permute-done = bf16[4,64,768]{2,1,0:T(8,128)(2,1)S(1)} collective-permute-done((bf16[4,64,768]{2,1,0:T(8,128)(2,1)S(1)}, bf16[4,64,768]{2,1,0:T(8,128)(2,1)S(1)}, u32[]{:S(2)}, u32[]{:S(2)}) %collective-permute-start) | collective-permute-done | bytes 393248 | tf_op jit(solution)/shard_map/ppermute | solution.py:454
  39.8 0.0 collective-permute-done.1
  39.8 0.9 pad_maximum_fusion.tok_halo
  40.8 6.3 %collective-permute-done.2 = bf16[4,64,768]{2,1,0:T(8,128)(2,1)S(1)} collective-permute-done((bf16[4,64,768]{2,1,0:T(8,128)(2,1)S(1)}, bf16[4,64,768]{2,1,0:T(8,128)(2,1)S(1)}, u32[]{:S(2)}, u32[]{:S(2)}) %collective-permute-start.2) | collective-permute-done | bytes 393248 | tf_op jit(solution)/shard_map/ppermute | solution.py:454
  47.1 0.0 collective-permute-done.3
  47.1 1.0 pad_maximum_fusion.1.cot_halo
  48.1 76.5 %layer_rows.1 = (bf16[4,256,768]{2,1,0:T(8,128)(2,1)}, bf16[4,128,768]{2,1,0:T(8,128)(2,1)}, bf16[4,256,768]{2,1,0:T(8,128)(2,1)}, bf16[4,128,768]{2,1,0:T(8,128)(2,1)}, f32[64,768]{1,0:T(8,128)}) custom-call(s32[4,1,2048]{2,1,0:T(1,128)} %broadcast_in_dim.4.ids, bf16[4,256,768]{2,1,0:T(8,128)(2,1)} %tok.1, bf16[4,128,768]{2,1,0:T(8,128)(2,1)} %pad_maximum_fusion.tok_halo, ...), custom_call_target="tpu_custom_call" | custom-call | tf_op jit(solution)/shard_map/layer_rows/pallas_call | solution.py:481
  124.6 0.0 copy-start.4
  124.6 0.0 copy-start.1
  124.6 0.0 copy-start.2
  124.6 2.2 fusion.3
  126.8 4.4 %collective-permute-start.4 = (bf16[4,64,768]{2,1,0:T(8,128)(2,1)}, bf16[4,64,768]{2,1,0:T(8,128)(2,1)S(1)}, u32[]{:S(2)}, u32[]{:S(2)}) collective-permute-start(bf16[4,64,768]{2,1,0:T(8,128)(2,1)} %get-tuple-element.31), channel_id=1, source_target_pairs={{0,1},{1,2},{2,3},{3,4},{4,5},{5,6},{6,7},{8,9},{9,10},{10,11},{11... | collective-permute-start | bytes 1179656 | tf_op jit(solution)/shard_map/ppermute | solution.py:454
  131.2 1.3 collective-permute-start.5
  132.5 2.1 fusion.2
  134.6 5.7 %collective-permute-start.6 = (bf16[4,64,768]{2,1,0:T(8,128)(2,1)}, bf16[4,64,768]{2,1,0:T(8,128)(2,1)}, u32[]{:S(2)}, u32[]{:S(2)}) collective-permute-start(bf16[4,64,768]{2,1,0:T(8,128)(2,1)} %get-tuple-element.29), channel_id=1, source_target_pairs={{0,1},{1,2},{2,3},{3,4},{4,5},{5,6},{6,7},{8,9},{9,10},{10,11},{11... | collective-permute-start | bytes 1179656 | tf_op jit(solution)/shard_map/ppermute | solution.py:454
  140.3 1.3 collective-permute-start.7
  141.6 0.1 pad.7.clone
  141.7 0.0 copy-done.4
  141.7 0.7 slice.51
  142.3 0.0 all-reduce.3.cloned.1.call-update
  142.4 15.8 %collective-permute-done.4 = bf16[4,64,768]{2,1,0:T(8,128)(2,1)S(1)} collective-permute-done((bf16[4,64,768]{2,1,0:T(8,128)(2,1)}, bf16[4,64,768]{2,1,0:T(8,128)(2,1)S(1)}, u32[]{:S(2)}, u32[]{:S(2)}) %collective-permute-start.4) | collective-permute-done | bytes 393248 | tf_op jit(solution)/shard_map/ppermute | solution.py:454
  158.1 0.0 collective-permute-done.5
  158.1 6.6 %collective-permute-done.6 = bf16[4,64,768]{2,1,0:T(8,128)(2,1)} collective-permute-done((bf16[4,64,768]{2,1,0:T(8,128)(2,1)}, bf16[4,64,768]{2,1,0:T(8,128)(2,1)}, u32[]{:S(2)}, u32[]{:S(2)}) %collective-permute-start.6) | collective-permute-done | bytes 393248 | tf_op jit(solution)/shard_map/ppermute | solution.py:454
  164.8 0.0 collective-permute-done.7
  164.8 0.0 copy-done.1
  164.8 3.9 %maximum_add_fusion.1 = (bf16[4,256,768]{2,1,0:T(8,128)(2,1)}, bf16[4,256,768]{2,1,0:T(8,128)(2,1)}) fusion(bf16[4,256,768]{2,1,0:T(8,128)(2,1)S(1)} %copy-done.2, bf16[4,64,768]{2,1,0:T(8,128)(2,1)} %collective-permute-done.7, bf16[4,64,768]{2,1,0:T(8,128)(2,1)} %collective-permute-done.6, bf16[256]{0:T(256)(128)(2,1)S(1)} %pad.7.clone, ...), kind=kLoop, calls=%fused_computation.1 | loop fusion | flops 11796480 | bytes 7864832 | tf_op jit(solution)/shard_map/add | solution.py:517
  168.7 100.3 %all-reduce.3.cloned.1.call-done = f32[50,768]{1,0:T(8,128)} async-done(((f32[50,768]{1,0:T(8,128)}), f32[50,768]{1,0:T(8,128)}) %all-reduce.3.cloned.1.call-update) | async-done | bytes 153616 | tf_op jit(solution)/shard_map/psum | solution.py:521
  269.0 1.6 copy.20
  (2 shorter events, 0.0 us)
Async XLA Ops:
  7.2 7.7 %copy-start = (bf16[4,256,768]{2,1,0:T(8,128)(2,1)S(1)}, bf16[4,256,768]{2,1,0:T(8,128)(2,1)}, u32[]{:S(2)}) copy-start(bf16[4,256,768]{2,1,0:T(8,128)(2,1)} %cot.1) | copy-start | bytes 4718596
  7.2 13.6 %copy-start.7 = (f32[768]{0:T(1024)S(1)}, f32[768]{0:T(1024)}, u32[]{:S(2)}) copy-start(f32[768]{0:T(1024)} %param.22) | copy-start | bytes 9220
  7.2 14.2 %copy-start.8 = (f32[768]{0:T(1024)S(1)}, f32[768]{0:T(1024)}, u32[]{:S(2)}) copy-start(f32[768]{0:T(1024)} %param.23) | copy-start | bytes 9220
  7.2 14.8 %copy-start.9 = (f32[768]{0:T(1024)S(1)}, f32[768]{0:T(1024)}, u32[]{:S(2)}) copy-start(f32[768]{0:T(1024)} %param.27) | copy-start | bytes 9220
  7.2 15.4 %copy-start.10 = (f32[768]{0:T(1024)S(1)}, f32[768]{0:T(1024)}, u32[]{:S(2)}) copy-start(f32[768]{0:T(1024)} %param.28) | copy-start | bytes 9220
  7.2 16.0 %copy-start.11 = (f32[768]{0:T(1024)S(1)}, f32[768]{0:T(1024)}, u32[]{:S(2)}) copy-start(f32[768]{0:T(1024)} %param.29) | copy-start | bytes 9220
  7.2 16.5 %copy-start.12 = (f32[768]{0:T(1024)S(1)}, f32[768]{0:T(1024)}, u32[]{:S(2)}) copy-start(f32[768]{0:T(1024)} %param.33) | copy-start | bytes 9220
  7.2 17.1 %copy-start.6 = (f32[1536]{0:T(1024)S(1)}, f32[1536]{0:T(1024)}, u32[]{:S(2)}) copy-start(f32[1536]{0:T(1024)} %param.25) | copy-start | bytes 18436
  7.2 17.7 %copy-start.5 = (s32[4,2048]{1,0:T(4,128)S(1)}, s32[4,2048]{1,0:T(4,128)}, u32[]{:S(2)}) copy-start(s32[4,2048]{1,0:T(4,128)} %param.21) | copy-start | bytes 98308
  7.3 18.3 %copy-start.3 = (f32[50,768]{1,0:T(8,128)S(1)}, f32[50,768]{1,0:T(8,128)}, u32[]{:S(2)}) copy-start(f32[50,768]{1,0:T(8,128)} %param.20) | copy-start | bytes 460804
  7.3 261.7 %all-reduce.3.cloned.1.call-start = ((), (), s32[]{:S(2)}) async-start(), calls=%async_computation | async-start | bytes 344064 | tf_op jit(solution)/shard_map/psum | solution.py:521
  8.6 31.2 %collective-permute-start = (bf16[4,64,768]{2,1,0:T(8,128)(2,1)S(1)}, bf16[4,64,768]{2,1,0:T(8,128)(2,1)S(1)}, u32[]{:S(2)}, u32[]{:S(2)}) collective-permute-start(bf16[4,64,768]{2,1,0:T(8,128)(2,1)S(1)} %get-tuple-element.27), channel_id=1, source_target_pairs={{0,1},{1,2},{2,3},{3,4},{4,5},{5,6},{6,7},{8,9},{9,10},{10,11},{11... | collective-permute-start | bytes 1179656 | tf_op jit(solution)/shard_map/ppermute | solution.py:454
  13.5 26.3 %collective-permute-start.1 = (bf16[4,64,768]{2,1,0:T(8,128)(2,1)S(1)}, bf16[4,64,768]{2,1,0:T(8,128)(2,1)S(1)}, u32[]{:S(2)}, u32[]{:S(2)}) collective-permute-start(bf16[4,64,768]{2,1,0:T(8,128)(2,1)S(1)} %get-tuple-element.28), channel_id=1, source_target_pairs={{1,0},{2,1},{3,2},{4,3},{5,4},{6,5},{7,6},{9,8},{10,9},{11,10},{12... | collective-permute-start | bytes 1179656 | tf_op jit(solution)/shard_map/ppermute | solution.py:453
  14.9 32.2 %collective-permute-start.2 = (bf16[4,64,768]{2,1,0:T(8,128)(2,1)S(1)}, bf16[4,64,768]{2,1,0:T(8,128)(2,1)S(1)}, u32[]{:S(2)}, u32[]{:S(2)}) collective-permute-start(bf16[4,64,768]{2,1,0:T(8,128)(2,1)S(1)} %get-tuple-element.25), channel_id=1, source_target_pairs={{0,1},{1,2},{2,3},{3,4},{4,5},{5,6},{6,7},{8,9},{9,10},{10,11},{11... | collective-permute-start | bytes 1179656 | tf_op jit(solution)/shard_map/ppermute | solution.py:454
  19.5 27.7 %collective-permute-start.3 = (bf16[4,64,768]{2,1,0:T(8,128)(2,1)S(1)}, bf16[4,64,768]{2,1,0:T(8,128)(2,1)S(1)}, u32[]{:S(2)}, u32[]{:S(2)}) collective-permute-start(bf16[4,64,768]{2,1,0:T(8,128)(2,1)S(1)} %get-tuple-element.26), channel_id=1, source_target_pairs={{1,0},{2,1},{3,2},{4,3},{5,4},{6,5},{7,6},{9,8},{10,9},{11,10},{12... | collective-permute-start | bytes 1179656 | tf_op jit(solution)/shard_map/ppermute | solution.py:453
  124.6 17.1 %copy-start.4 = (f32[64,768]{1,0:T(8,128)S(1)}, f32[64,768]{1,0:T(8,128)}, u32[]{:S(2)}) copy-start(f32[64,768]{1,0:T(8,128)} %get-tuple-element.24) | copy-start | bytes 589828
  124.6 40.2 %copy-start.1 = (bf16[4,256,768]{2,1,0:T(8,128)(2,1)S(1)}, bf16[4,256,768]{2,1,0:T(8,128)(2,1)}, u32[]{:S(2)}) copy-start(bf16[4,256,768]{2,1,0:T(8,128)(2,1)} %get-tuple-element.20) | copy-start | bytes 4718596
  124.6 40.2 %copy-start.2 = (bf16[4,256,768]{2,1,0:T(8,128)(2,1)S(1)}, bf16[4,256,768]{2,1,0:T(8,128)(2,1)}, u32[]{:S(2)}) copy-start(bf16[4,256,768]{2,1,0:T(8,128)(2,1)} %get-tuple-element.22) | copy-start | bytes 4718596
  126.8 31.3 %collective-permute-start.4 = (bf16[4,64,768]{2,1,0:T(8,128)(2,1)}, bf16[4,64,768]{2,1,0:T(8,128)(2,1)S(1)}, u32[]{:S(2)}, u32[]{:S(2)}) collective-permute-start(bf16[4,64,768]{2,1,0:T(8,128)(2,1)} %get-tuple-element.31), channel_id=1, source_target_pairs={{0,1},{1,2},{2,3},{3,4},{4,5},{5,6},{6,7},{8,9},{9,10},{10,11},{11... | collective-permute-start | bytes 1179656 | tf_op jit(solution)/shard_map/ppermute | solution.py:454
  131.2 26.9 %collective-permute-start.5 = (bf16[4,64,768]{2,1,0:T(8,128)(2,1)}, bf16[4,64,768]{2,1,0:T(8,128)(2,1)}, u32[]{:S(2)}, u32[]{:S(2)}) collective-permute-start(bf16[4,64,768]{2,1,0:T(8,128)(2,1)} %get-tuple-element.32), channel_id=1, source_target_pairs={{1,0},{2,1},{3,2},{4,3},{5,4},{6,5},{7,6},{9,8},{10,9},{11,10},{12... | collective-permute-start | bytes 1179656 | tf_op jit(solution)/shard_map/ppermute | solution.py:453
  134.6 30.2 %collective-permute-start.6 = (bf16[4,64,768]{2,1,0:T(8,128)(2,1)}, bf16[4,64,768]{2,1,0:T(8,128)(2,1)}, u32[]{:S(2)}, u32[]{:S(2)}) collective-permute-start(bf16[4,64,768]{2,1,0:T(8,128)(2,1)} %get-tuple-element.29), channel_id=1, source_target_pairs={{0,1},{1,2},{2,3},{3,4},{4,5},{5,6},{6,7},{8,9},{9,10},{10,11},{11... | collective-permute-start | bytes 1179656 | tf_op jit(solution)/shard_map/ppermute | solution.py:454
  140.3 24.5 %collective-permute-start.7 = (bf16[4,64,768]{2,1,0:T(8,128)(2,1)}, bf16[4,64,768]{2,1,0:T(8,128)(2,1)}, u32[]{:S(2)}, u32[]{:S(2)}) collective-permute-start(bf16[4,64,768]{2,1,0:T(8,128)(2,1)} %get-tuple-element.30), channel_id=1, source_target_pairs={{1,0},{2,1},{3,2},{4,3},{5,4},{6,5},{7,6},{9,8},{10,9},{11,10},{12... | collective-permute-start | bytes 1179656 | tf_op jit(solution)/shard_map/ppermute | solution.py:453
Sparse Core Ops, SparseCore 0:
  142.5 126.4 all-reduce.2

commit v2 on v1

--- a/solution.py
+++ b/solution.py
@@ -231,6 +231,7 @@
     return (output, token_gradient, prompt_gradient)
 
 
+MESH = pl.DeviceIdType.MESH
 HALO = 64
 SLOTS = 320
 KEYS = 256
@@ -294,23 +295,124 @@
     return jnp.where((place >= start) & (place < end), place - start, slot)
 
 
+def needed(tokens):
+    return (tokens + 15) // 16 * 16
+
+
+def sized(count, act):
+    for size in range(16, HALO + 1, 16):
+        pl.when(count == size)(functools.partial(act, size))
+
+
 def row_kernel(
-    ids, tok, tok_halo, cot, cot_halo, prom, g1, b1, w_qkv, b_qv, w_out, b_out, g2, b2, w_up, b_up, w_down, b_down,
-    out, out_halo, tgr, tgr_halo, pgr,
-    pick, ins, n1, inv1, wide, qkv, probs, turned, hid, n2, inv2, act, upg, og, grad,
+    ids, tok, cot, tok_all, cot_all, prompts, g1, b1, w_qkv_hbm, b_qv, w_out_hbm, b_out, g2, b2, w_up_hbm, b_up,
+    w_down_hbm, b_down,
+    out, tgr, pgr,
+    w_qkv, w_out, w_up, w_down, w_sem,
+    prom, pick, ins, n1, inv1, wide, qkv, probs, turned, hid, n2, inv2, act, upg, og, grad,
+    halos, halo_send, halo_recv, sides, backs, side_send, side_recv,
+    part, part_in, part_send, part_recv,
 ):
     index = lax.axis_index("seq")
+    group = lax.axis_index("batch")
+    row = pl.program_id(0)
+    rows = tok_all.shape[0]
     span, width = tok.shape[1], tok.shape[2]
     ff = w_up.shape[1]
     bf = jnp.bfloat16
-    slot = slot_map(ids[0], index, span)
+    last = IMAGES_PER_ROW - 1
+    slack = span - IMAGE_TOKENS
+    has_left, has_right = index > 0, index < last
+    from_left = jnp.where(has_left, needed(slack * index), 0)
+    from_right = jnp.where(has_right, needed(slack * (last - index)), 0)
+    to_right = jnp.where(has_right, needed(slack * (index + 1)), 0)
+    to_left = jnp.where(has_left, needed(slack * (IMAGES_PER_ROW - index)), 0)
+
+    def weight(k):
+        source = (w_qkv_hbm, w_out_hbm, w_up_hbm, w_down_hbm)[k]
+        return pltpu.make_async_copy(source, (w_qkv, w_out, w_up, w_down)[k], w_sem.at[k])
+
+    def arrived(k):
+        pl.when(row == 0)(lambda: weight(k).wait())
+
+    def seq_copy(source, target, send, recv, to):
+        return pltpu.make_async_remote_copy(
+            source, target, send, recv, device_id={"seq": to}, device_id_type=MESH
+        )
+
+    def halo_right(kind, r, size):
+        source = (tok_all, cot_all)[kind].at[r, span - size :]
+        target = halos.at[kind, r, HALO - size : HALO]
+        return seq_copy(source, target, halo_send.at[kind, r, 0], halo_recv.at[kind, r, 0], index + 1)
+
+    def halo_left(kind, r, size):
+        source = (tok_all, cot_all)[kind].at[r, :size]
+        target = halos.at[kind, r, HALO : HALO + size]
+        return seq_copy(source, target, halo_send.at[kind, r, 1], halo_recv.at[kind, r, 1], index - 1)
+
+    def halo_wait(kind, r):
+        sized(from_left, lambda size: halo_right(kind, r, size).wait_recv())
+        sized(from_right, lambda size: halo_left(kind, r, size).wait_recv())
+
+    def side_left(kind, r, size):
+        source = sides.at[kind, r, HALO - size : HALO]
+        target = backs.at[kind, r, 2 * HALO - size :]
+        return seq_copy(source, target, side_send.at[kind, r, 0], side_recv.at[kind, r, 0], index - 1)
+
+    def side_right(kind, r, size):
+        source = sides.at[kind, r, HALO : HALO + size]
+        target = backs.at[kind, r, :size]
+        return seq_copy(source, target, side_send.at[kind, r, 1], side_recv.at[kind, r, 1], index + 1)
+
+    def side_start(kind, r):
+        sized(from_left, lambda size: side_left(kind, r, size).start())
+        sized(from_right, lambda size: side_right(kind, r, size).start())
+
+    def side_merge(kind, r):
+        sized(to_right, lambda size: side_left(kind, r, size).wait_recv())
+        sized(to_left, lambda size: side_right(kind, r, size).wait_recv())
+        result = (out, tgr)[kind]
+        result[r, :HALO] = result[r, :HALO] + backs[kind, r, :HALO]
+        result[r, span - HALO :] = result[r, span - HALO :] + backs[kind, r, HALO:]
+
+    def flipped(place, step):
+        return place + step - 2 * step * (place // step % 2)
+
+    partners = tuple({"batch": flipped(group, k)} for k in (1, 2)) + tuple({"seq": flipped(index, k)} for k in (1, 2, 4))
+
+    @pl.when(row == 0)
+    def _():
+        for k in range(4):
+            weight(k).start()
+        halos[...] = jnp.zeros_like(halos)
+        backs[...] = jnp.zeros_like(backs)
+        barrier = pltpu.get_barrier_semaphore()
+        for device in partners:
+            pl.semaphore_signal(barrier, inc=1, device_id=device, device_id_type=MESH)
+        @pl.when(has_left)
+        def _():
+            pl.semaphore_signal(barrier, inc=1, device_id={"seq": index - 1}, device_id_type=MESH)
+        @pl.when(has_right)
+        def _():
+            pl.semaphore_signal(barrier, inc=1, device_id={"seq": index + 1}, device_id_type=MESH)
+        prom[...] = jnp.zeros_like(prom)
+        prom[1 : PROMPTS + 1] = prompts[...]
+        part[...] = jnp.zeros_like(part)
+        pl.semaphore_wait(barrier, len(partners) + jnp.where(has_left, 1, 0) + jnp.where(has_right, 1, 0))
+        for r in range(rows):
+            for kind in range(2):
+                sized(to_right, lambda size: halo_right(kind, r, size).start())
+                sized(to_left, lambda size: halo_left(kind, r, size).start())
+
+    slot = slot_map(ids[pl.ds(row, 1)], index, span)
     slots = lax.broadcasted_iota(jnp.int32, (SLOTS, span + 2 * HALO), 0)
     pick[...] = jnp.where(slots == slot, 1.0, 0.0).astype(bf)
 
     first_rows = lax.broadcasted_iota(jnp.int32, (64, 1), 0)
     is_prompt = (first_rows >= 1) & (first_rows <= PROMPTS)
+    halo_wait(0, row)
     for r in range(0, SLOTS, 64):
-        x = dot(pick[r : r + 64, :span], tok[0]) + dot(pick[r : r + 64, span:], tok_halo[0])
+        x = dot(pick[r : r + 64, :span], tok[0]) + dot(pick[r : r + 64, span:], halos[0, row])
         if r == 0:
             x = jnp.where(is_prompt, prom[...], x)
         ins[r : r + 64] = x
@@ -321,14 +423,15 @@
         if r < KEYS:
             n1[r : r + 64] = c
             inv1[r : r + 64] = inv
-        wide[r : r + 64] = (c * g1[...] + b1[...]).astype(bf)
-
+        wide[r : r + 64] = (c * g1[...][None] + b1[...][None]).astype(bf)
+
+    arrived(0)
     for c in range(0, width, 256):
-        q = dot(wide[:KEYS], w_qkv[:, c : c + 256]) + b_qv[:, c : c + 256]
+        q = dot(wide[:KEYS], w_qkv[:, c : c + 256]) + b_qv[c : c + 256][None]
         qkv[:KEYS, c : c + 256] = (q * SCALE).astype(bf)
         k = dot(wide[:KEYS], w_qkv[:, width + c : width + c + 256])
         qkv[:KEYS, width + c : width + c + 256] = k.astype(bf)
-        v = dot(wide[...], w_qkv[:, 2 * width + c : 2 * width + c + 256]) + b_qv[:, width + c : width + c + 256]
+        v = dot(wide[...], w_qkv[:, 2 * width + c : 2 * width + c + 256]) + b_qv[width + c : width + c + 256][None]
         qkv[:, 2 * width + c : 2 * width + c + 256] = v.astype(bf)
 
     lane = lax.broadcasted_iota(jnp.int32, (1, PAIR), 1)
@@ -365,8 +468,9 @@
     attended = turned[...].T
     wide[:KEYS] = jnp.where(key_rows < IMAGE_TOKENS, attended, qkv[:KEYS, 2 * width :])
     wide[KEYS:] = qkv[KEYS:, 2 * width :]
+    arrived(1)
     for c in range(0, width, 256):
-        hid[:, c : c + 256] = ins[:, c : c + 256] + dot(wide[...], w_out[:, c : c + 256]) + b_out[:, c : c + 256]
+        hid[:, c : c + 256] = ins[:, c : c + 256] + dot(wide[...], w_out[:, c : c + 256]) + b_out[c : c + 256][None]
 
     for r in range(0, SLOTS, 64):
         x = hid[r : r + 64]
@@ -377,36 +481,41 @@
         if r < KEYS:
             n2[r : r + 64] = c
             inv2[r : r + 64] = inv
-        wide[r : r + 64] = (c * g2[...] + b2[...]).astype(bf)
+        wide[r : r + 64] = (c * g2[...][None] + b2[...][None]).astype(bf)
+    halo_wait(1, row)
     for r in range(0, KEYS, 64):
-        x = dot(pick[r : r + 64, :span], cot[0]) + dot(pick[r : r + 64, span:], cot_halo[0])
+        x = dot(pick[r : r + 64, :span], cot[0]) + dot(pick[r : r + 64, span:], halos[1, row])
         if r + 64 == KEYS:
             x = jnp.where(first_rows < IMAGE_TOKENS - r, x, 0.0)
         og[r : r + 64] = x.astype(bf)
 
+    arrived(2)
+    arrived(3)
     for c in range(0, ff, 256):
-        upper = dot(wide[...], w_up[:, c : c + 256]) + b_up[:, c : c + 256]
+        upper = dot(wide[...], w_up[:, c : c + 256]) + b_up[c : c + 256][None]
         act_grad = dot_nt(og[...], w_down[c : c + 256, :])
         value, slope = gelu_parts(upper)
         act[:, c : c + 256] = value.astype(bf)
         upg[:, c : c + 256] = (act_grad * slope[:KEYS]).astype(bf)
     for c in range(0, width, 256):
-        y = hid[:, c : c + 256] + dot(act[...], w_down[:, c : c + 256]) + b_down[:, c : c + 256]
+        y = hid[:, c : c + 256] + dot(act[...], w_down[:, c : c + 256]) + b_down[c : c + 256][None]
         wide[:, c : c + 256] = y.astype(bf)
         grad[:, c : c + 256] = dot_nt(upg[...], w_up[c : c + 256, :])
-    out[0] = dot_tn(pick[:, :span], wide[...]).astype(bf)
-    out_halo[0] = dot_tn(pick[:, span:], wide[...]).astype(bf)
+    out[row] = dot_tn(pick[:, :span], wide[...]).astype(bf)
+    sides[0, row] = dot_tn(pick[:, span:], wide[...]).astype(bf)
 
     for r in range(0, KEYS, 64):
-        e = grad[r : r + 64] * g2[...]
+        e = grad[r : r + 64] * g2[...][None]
         n = n2[r : r + 64]
         mean = jnp.mean(e, axis=-1, keepdims=True)
-        part = jnp.mean(e * n, axis=-1, keepdims=True)
-        h = og[r : r + 64].astype(jnp.float32) + inv2[r : r + 64] * (e - mean - n * part)
+        lean = jnp.mean(e * n, axis=-1, keepdims=True)
+        h = og[r : r + 64].astype(jnp.float32) + inv2[r : r + 64] * (e - mean - n * lean)
         hid[r : r + 64] = h
         wide[r : r + 64] = h.astype(bf)
     for c in range(0, width, 256):
         og[:, c : c + 256] = dot_nt(wide[:KEYS], w_out[c : c + 256, :]).astype(bf)
+
+    side_start(0, row)
 
     for p in range(width // PAIR):
         at = p * PAIR
@@ -429,30 +538,70 @@
     for c in range(0, width, 256):
         grad[:, c : c + 256] = dot_nt(qkv[:KEYS], w_qkv[c : c + 256, :])
     for r in range(0, KEYS, 64):
-        e = grad[r : r + 64] * g1[...]
+        e = grad[r : r + 64] * g1[...][None]
         n = n1[r : r + 64]
         mean = jnp.mean(e, axis=-1, keepdims=True)
-        part = jnp.mean(e * n, axis=-1, keepdims=True)
-        x = hid[r : r + 64] + inv1[r : r + 64] * (e - mean - n * part)
+        lean = jnp.mean(e * n, axis=-1, keepdims=True)
+        x = hid[r : r + 64] + inv1[r : r + 64] * (e - mean - n * lean)
         if r == 0:
-            @pl.when(pl.program_id(0) == 0)
-            def _():
-                pgr[...] = x
-
-            @pl.when(pl.program_id(0) > 0)
-            def _():
-                pgr[...] += x
+            part[...] += x
             x = jnp.where(is_prompt, 0.0, x)
         wide[r : r + 64] = x.astype(bf)
-    tgr[0] = dot_tn(pick[:KEYS, :span], wide[:KEYS]).astype(bf)
-    tgr_halo[0] = dot_tn(pick[:KEYS, span:], wide[:KEYS]).astype(bf)
-
-
-def swapped(to_left, to_right):
-    count = lax.axis_size("seq")
-    from_right = lax.ppermute(to_left, "seq", [(i, i - 1) for i in range(1, count)])
-    from_left = lax.ppermute(to_right, "seq", [(i, i + 1) for i in range(count - 1)])
-    return from_left, from_right
+    tgr[row] = dot_tn(pick[:KEYS, :span], wide[:KEYS]).astype(bf)
+    sides[1, row] = dot_tn(pick[:KEYS, span:], wide[:KEYS]).astype(bf)
+
+    @pl.when(row > 0)
+    def _():
+        side_merge(0, row - 1)
+        side_merge(1, row - 1)
+
+    side_start(1, row)
+
+    @pl.when(row == rows - 1)
+    def _():
+        def exchange(stage, source, target):
+            partner = partners[(0, 1, 2, 3, 4, 2, 1, 0)[stage]]
+            copy = pltpu.make_async_remote_copy(
+                source, target, part_send.at[stage], part_recv.at[stage], device_id=partner, device_id_type=MESH
+            )
+            copy.start()
+            copy.wait()
+
+        def rows_at(first, size):
+            return pl.ds(pl.multiple_of(first, 8), size)
+
+        first = 0
+        size = part.shape[0]
+        kept = []
+        base = 0
+        for stage, bit in enumerate((group % 2, group // 2, index % 2)):
+            size = size // 2
+            kept.append((first, size, bit))
+            landed = part_in.at[base : base + size]
+            exchange(stage, part.at[rows_at(first + (1 - bit) * size, size)], landed)
+            first = first + bit * size
+            part[rows_at(first, size)] += landed[...]
+            base += size
+        for stage in (3, 4):
+            landed = part_in.at[base : base + size]
+            exchange(stage, part.at[rows_at(first, size)], landed)
+            part[rows_at(first, size)] += landed[...]
+            base += size
+        for stage in (5, 6, 7):
+            before, size, bit = kept[7 - stage]
+            landed = part_in.at[base : base + size]
+            exchange(stage, part.at[rows_at(before + bit * size, size)], landed)
+            part[rows_at(before + (1 - bit) * size, size)] = landed[...]
+            base += size
+        pgr[...] = part[1 : PROMPTS + 1]
+        side_merge(0, row)
+        side_merge(1, row)
+        for r in range(rows):
+            for kind in range(2):
+                sized(to_right, lambda size: halo_right(kind, r, size).wait_send())
+                sized(to_left, lambda size: halo_left(kind, r, size).wait_send())
+                sized(from_left, lambda size: side_left(kind, r, size).wait_send())
+                sized(from_right, lambda size: side_right(kind, r, size).wait_send())
 
 
 def image_body(
@@ -460,70 +609,58 @@
     ln2_gain, ln2_bias, w_up, bias_up, w_down, bias_down, cotangent,
 ):
     rows, span, width = tokens.shape
-    length = image_id.shape[1]
     ff = w_up.shape[1]
     f32, bf = jnp.float32, jnp.bfloat16
-
-    def halo(x):
-        return jnp.concatenate(swapped(x[:, :HALO], x[:, span - HALO :]), axis=1)
-
-    prom = jnp.zeros((64, width), f32).at[1 : PROMPTS + 1].set(prompts)
-
-    def per_row(*shape):
-        return pl.BlockSpec((1,) + shape, lambda r: (r, 0, 0))
-
-    def whole(*shape):
-        return pl.BlockSpec(shape, lambda r: (0,) * len(shape), pipeline_mode=pl.Buffered(1))
-
-    def line(x):
-        return x.reshape(1, -1)
-
-    out, out_halo, tgr, tgr_halo, pgr = pl.pallas_call(
+    dma = pltpu.SemaphoreType.DMA
+
+    per_row = pl.BlockSpec((1, span, width), lambda r: (r, 0, 0))
+    in_place = pl.BlockSpec(memory_space=pl.ANY)
+
+    def whole(array):
+        return pl.BlockSpec(array.shape, lambda r: (0,) * len(array.shape), pipeline_mode=pl.Buffered(1))
+
+    return pl.pallas_call(
         row_kernel,
         grid=(rows,),
         in_specs=[
-            per_row(1, length), per_row(span, width), per_row(2 * HALO, width), per_row(span, width),
-            per_row(2 * HALO, width), whole(64, width), whole(1, width), whole(1, width), whole(width, 3 * width),
-            whole(1, 2 * width), whole(width, width), whole(1, width), whole(1, width), whole(1, width),
-            whole(width, ff), whole(1, ff), whole(ff, width), whole(1, width),
+            whole(image_id), per_row, per_row, in_place, in_place, whole(prompts), whole(ln1_gain), whole(ln1_bias),
+            in_place, whole(bias_qv), in_place, whole(bias_out), whole(ln2_gain), whole(ln2_bias), in_place,
+            whole(bias_up), in_place, whole(bias_down),
         ],
         out_specs=[
-            per_row(span, width), per_row(2 * HALO, width), per_row(span, width), per_row(2 * HALO, width),
-            pl.BlockSpec((64, width), lambda r: (0, 0)),
+            pl.BlockSpec((rows, span, width), lambda r: (0, 0, 0)), pl.BlockSpec((rows, span, width), lambda r: (0, 0, 0)),
+            pl.BlockSpec((PROMPTS, width), lambda r: (0, 0)),
         ],
         out_shape=[
-            jax.ShapeDtypeStruct((rows, span, width), bf), jax.ShapeDtypeStruct((rows, 2 * HALO, width), bf),
-            jax.ShapeDtypeStruct((rows, span, width), bf), jax.ShapeDtypeStruct((rows, 2 * HALO, width), bf),
-            jax.ShapeDtypeStruct((64, width), f32),
+            jax.ShapeDtypeStruct((rows, span, width), bf), jax.ShapeDtypeStruct((rows, span, width), bf),
+            jax.ShapeDtypeStruct((PROMPTS, width), f32),
         ],
         scratch_shapes=[
-            pltpu.VMEM((SLOTS, span + 2 * HALO), bf), pltpu.VMEM((SLOTS, width), f32), pltpu.VMEM((KEYS, width), f32),
-            pltpu.VMEM((KEYS, 1), f32), pltpu.VMEM((SLOTS, width), bf), pltpu.VMEM((SLOTS, 3 * width), bf),
-            pltpu.VMEM((width // PAIR, KEYS, 2 * KEYS), bf), pltpu.VMEM((width, KEYS), bf),
-            pltpu.VMEM((SLOTS, width), f32), pltpu.VMEM((KEYS, width), f32), pltpu.VMEM((KEYS, 1), f32),
-            pltpu.VMEM((SLOTS, ff), bf), pltpu.VMEM((KEYS, ff), bf), pltpu.VMEM((KEYS, width), bf),
-            pltpu.VMEM((KEYS, width), f32),
+            pltpu.VMEM(w_qkv.shape, bf), pltpu.VMEM(w_out.shape, bf), pltpu.VMEM(w_up.shape, bf),
+            pltpu.VMEM(w_down.shape, bf), dma((4,)),
+            pltpu.VMEM((64, width), f32), pltpu.VMEM((SLOTS, span + 2 * HALO), bf), pltpu.VMEM((SLOTS, width), f32),
+            pltpu.VMEM((KEYS, width), f32), pltpu.VMEM((KEYS, 1), f32), pltpu.VMEM((SLOTS, width), bf),
+            pltpu.VMEM((SLOTS, 3 * width), bf), pltpu.VMEM((width // PAIR, KEYS, 2 * KEYS), bf),
+            pltpu.VMEM((width, KEYS), bf), pltpu.VMEM((SLOTS, width), f32), pltpu.VMEM((KEYS, width), f32),
+            pltpu.VMEM((KEYS, 1), f32), pltpu.VMEM((SLOTS, ff), bf), pltpu.VMEM((KEYS, ff), bf),
+            pltpu.VMEM((KEYS, width), bf), pltpu.VMEM((KEYS, width), f32),
+            pltpu.VMEM((2, rows, 2 * HALO, width), bf), dma((2, rows, 2)), dma((2, rows, 2)),
+            pltpu.VMEM((2, rows, 2 * HALO, width), bf), pltpu.VMEM((2, rows, 2 * HALO, width), bf),
+            dma((2, rows, 2)), dma((2, rows, 2)),
+            pltpu.VMEM((64, width), f32), pltpu.VMEM((128, width), f32), dma((8,)), dma((8,)),
         ],
-        compiler_params=pltpu.CompilerParams(vmem_limit_bytes=60 << 20, dimension_semantics=("arbitrary",)),
+        compiler_params=pltpu.CompilerParams(
+            vmem_limit_bytes=62 << 20, dimension_semantics=("arbitrary",), collective_id=0, has_side_effects=True
+        ),
         name="layer_rows",
     )(
-        image_id[:, None], tokens, halo(tokens), cotangent, halo(cotangent), prom, line(ln1_gain), line(ln1_bias),
-        w_qkv, line(bias_qv), w_out, line(bias_out), line(ln2_gain), line(ln2_bias), w_up, line(bias_up), w_down,
-        line(bias_down),
-    )
-
-    def home(own, sides):
-        from_left, from_right = swapped(sides[:, :HALO], sides[:, HALO:])
-        return own + jnp.concatenate(
-            [from_left, jnp.zeros((rows, span - 2 * HALO, width), bf), from_right], axis=1
-        )
-
-    prompt_gradient = lax.psum(pgr[1 : PROMPTS + 1], ("batch", "seq"))
-    return home(out, out_halo), home(tgr, tgr_halo), prompt_gradient
+        image_id, tokens, cotangent, tokens, cotangent, prompts, ln1_gain, ln1_bias, w_qkv, bias_qv, w_out, bias_out,
+        ln2_gain, ln2_bias, w_up, bias_up, w_down, bias_down,
+    )
 
 
 def body(tokens, prompts, image_id, *rest):
-    if lax.axis_size("seq") == IMAGES_PER_ROW and tokens.shape[1] == KEYS:
+    if lax.axis_size("seq") == IMAGES_PER_ROW and lax.axis_size("batch") == 4 and tokens.shape[1] == KEYS:
         return image_body(tokens, prompts, image_id, *rest)
     return general_body(tokens, prompts, image_id, *rest)
 

time: 279 us -> 128 us (0.46)
  waiting for transfers between devices: 143 us -> 0 us
  Pallas kernels: 76.5 us -> 123 us
  starting transfers between devices: 24.7 us -> 0 us
  between operations: 14.2 us -> 0.66 us
  local copies, waits for them, and re-layouts: 13.5 us -> 4.59 us
  other arithmetic: 5.82 us -> 0 us
    psum x1 -> x0, waiting for transfers between devices: 100 us -> none  [image_body(): prompt_gradient = lax.psum(pgr[1:PROMPTS + 1], ('batch', 'seq'))]
    pallas_call x1, Pallas kernels: 76.5 us -> 123 us  [image_body(): pl.pallas_call(row_kernel, grid=(rows,), in_specs=[whole(image_id), per_r...]
    ppermute x8 -> x0, waiting for transfers between devices: 42.3 us -> none  [the longest x4 42.3 us: swapped(): lax.ppermute(to_right, 'seq', [(i, i + 1) for i in range(count - 1)])]
    ppermute x8 -> x0, starting transfers between devices: 24.7 us -> none  [the longest x4 19.6 us: swapped(): lax.ppermute(to_right, 'seq', [(i, i + 1) for i in range(count - 1)])]
    slice x5 -> x0, local copies, waits for them, and re-layouts: 6.29 us -> none  [the longest x2 4.28 us: home(): from_left, from_right = swapped(sides[:, :HALO], sides[:, HALO:])]
    reshape x7 -> x0, local copies, waits for them, and re-layouts: 4.15 us -> none  [line(): return x.reshape(1, -1)]
    add x1 -> x0, other arithmetic: 3.91 us -> none  [home(): own + jnp.concatenate([from_left, jnp.zeros((rows, span - 2 * HALO, width...]
    unnamed x27 -> x7, local copies, waits for them, and re-layouts: 1.66 us -> 4.59 us
  transfers between devices with their start and end apart: 9 -> 0, of which waited for: 5 -> 0; matrix products, arithmetic and copies ran while one was open for 5% -> 0% of each run, Pallas kernels for 0% -> 0%
where the time goes in v2:
time: 128 us
  Pallas kernels  123 us (96%)
  local copies, waits for them, and re-layouts  4.59 us (4%)
    pallas_call x1, Pallas kernels, image_body(): pl.pallas_call(row_kernel, grid=(rows,), in_specs=[whole(image_id), per_r...  123 us
    unnamed x7, local copies, waits for them, and re-layouts  4.59 us

profile of v2, /device:TPU:0, one launch (start us, length us, event | category | flops | bytes accessed | tf_op | source)
XLA Modules:
  0.0 128.2 jit_solution(12954978887826774145)
XLA Ops:
  0.6 122.9 %layer_rows.1 = (bf16[4,256,768]{2,1,0:T(8,128)(2,1)}, bf16[4,256,768]{2,1,0:T(8,128)(2,1)}, f32[50,768]{1,0:T(8,128)}) custom-call(s32[4,2048]{1,0:T(4,128)} %ids.1, bf16[4,256,768]{2,1,0:T(8,128)(2,1)} %tok_all.1, bf16[4,256,768]{2,1,0:T(8,128)(2,1)} %cot_all.1, bf16[4,256,768]{2,1,0:T(8,128)(2,1)} %tok_all.1, bf16[4,256,768]{2,1,0:T(8,128)(2,1)} %cot_all.1, ...), custom_call_target="tpu_custom_call" | custom-call | tf_op jit(solution)/shard_map/layer_rows/pallas_call | solution.py:622
  123.6 0.0 copy-start
  123.6 2.8 %copy.22 = bf16[4,256,768]{2,1,0:T(8,128)(2,1)} copy(bf16[4,256,768]{2,1,0:T(8,128)(2,1)} %get-tuple-element.6) | data formatting | bytes 3145728
  126.3 0.0 copy-done
  126.3 0.0 copy-start.1
  126.3 1.1 copy.23
  127.5 0.0 copy-done.1
  127.5 0.7 copy.24
Async XLA Ops:
  123.6 2.8 %copy-start = (bf16[4,256,768]{2,1,0:T(8,128)(2,1)S(1)}, bf16[4,256,768]{2,1,0:T(8,128)(2,1)}, u32[]{:S(2)}) copy-start(bf16[4,256,768]{2,1,0:T(8,128)(2,1)} %get-tuple-element.7) | copy-start | bytes 4718596
  126.3 1.1 copy-start.1

commit v3 on v2

--- a/solution.py
+++ b/solution.py
@@ -350,6 +350,10 @@
         target = halos.at[kind, r, HALO : HALO + size]
         return seq_copy(source, target, halo_send.at[kind, r, 1], halo_recv.at[kind, r, 1], index - 1)
 
+    def halo_start(kind, r):
+        sized(to_right, lambda size: halo_right(kind, r, size).start())
+        sized(to_left, lambda size: halo_left(kind, r, size).start())
+
     def halo_wait(kind, r):
         sized(from_left, lambda size: halo_right(kind, r, size).wait_recv())
         sized(from_right, lambda size: halo_left(kind, r, size).wait_recv())
@@ -399,10 +403,7 @@
         prom[1 : PROMPTS + 1] = prompts[...]
         part[...] = jnp.zeros_like(part)
         pl.semaphore_wait(barrier, len(partners) + jnp.where(has_left, 1, 0) + jnp.where(has_right, 1, 0))
-        for r in range(rows):
-            for kind in range(2):
-                sized(to_right, lambda size: halo_right(kind, r, size).start())
-                sized(to_left, lambda size: halo_left(kind, r, size).start())
+        halo_start(0, 0)
 
     slot = slot_map(ids[pl.ds(row, 1)], index, span)
     slots = lax.broadcasted_iota(jnp.int32, (SLOTS, span + 2 * HALO), 0)
@@ -411,6 +412,7 @@
     first_rows = lax.broadcasted_iota(jnp.int32, (64, 1), 0)
     is_prompt = (first_rows >= 1) & (first_rows <= PROMPTS)
     halo_wait(0, row)
+    halo_start(1, row)
     for r in range(0, SLOTS, 64):
         x = dot(pick[r : r + 64, :span], tok[0]) + dot(pick[r : r + 64, span:], halos[0, row])
         if r == 0:
@@ -483,6 +485,7 @@
             inv2[r : r + 64] = inv
         wide[r : r + 64] = (c * g2[...][None] + b2[...][None]).astype(bf)
     halo_wait(1, row)
+    pl.when(row < rows - 1)(lambda: halo_start(0, row + 1))
     for r in range(0, KEYS, 64):
         x = dot(pick[r : r + 64, :span], cot[0]) + dot(pick[r : r + 64, span:], halos[1, row])
         if r + 64 == KEYS:

time: 128 us -> 115 us (0.90)
  Pallas kernels: 123 us -> 110 us
    pallas_call x1, Pallas kernels: 123 us -> 110 us  [image_body(): pl.pallas_call(row_kernel, grid=(rows,), in_specs=[whole(image_id), per_r...]
where the time goes in v3:
time: 115 us
  Pallas kernels  110 us (96%)
  local copies, waits for them, and re-layouts  4.59 us (4%)
    pallas_call x1, Pallas kernels, image_body(): pl.pallas_call(row_kernel, grid=(rows,), in_specs=[whole(image_id), per_r...  110 us
    unnamed x7, local copies, waits for them, and re-layouts  4.59 us

profile of v3, /device:TPU:0, one launch (start us, length us, event | category | flops | bytes accessed | tf_op | source)
XLA Modules:
  0.0 114.8 jit_solution(11824917063786065589)
XLA Ops:
  0.6 109.5 %layer_rows.1 = (bf16[4,256,768]{2,1,0:T(8,128)(2,1)}, bf16[4,256,768]{2,1,0:T(8,128)(2,1)}, f32[50,768]{1,0:T(8,128)}) custom-call(s32[4,2048]{1,0:T(4,128)} %ids.1, bf16[4,256,768]{2,1,0:T(8,128)(2,1)} %tok_all.1, bf16[4,256,768]{2,1,0:T(8,128)(2,1)} %cot_all.1, bf16[4,256,768]{2,1,0:T(8,128)(2,1)} %tok_all.1, bf16[4,256,768]{2,1,0:T(8,128)(2,1)} %cot_all.1, ...), custom_call_target="tpu_custom_call" | custom-call | tf_op jit(solution)/shard_map/layer_rows/pallas_call | solution.py:625
  110.2 0.0 copy-start
  110.2 2.8 %copy.22 = bf16[4,256,768]{2,1,0:T(8,128)(2,1)} copy(bf16[4,256,768]{2,1,0:T(8,128)(2,1)} %get-tuple-element.6) | data formatting | bytes 3145728
  112.9 0.0 copy-done
  112.9 0.0 copy-start.1
  112.9 1.1 copy.23
  114.1 0.0 copy-done.1
  114.1 0.7 copy.24
Async XLA Ops:
  110.2 2.8 %copy-start = (bf16[4,256,768]{2,1,0:T(8,128)(2,1)S(1)}, bf16[4,256,768]{2,1,0:T(8,128)(2,1)}, u32[]{:S(2)}) copy-start(bf16[4,256,768]{2,1,0:T(8,128)(2,1)} %get-tuple-element.7) | copy-start | bytes 4718596
  112.9 1.1 copy-start.1

commit v4 on v3

--- a/solution.py
+++ b/solution.py
@@ -233,7 +233,7 @@
 
 MESH = pl.DeviceIdType.MESH
 HALO = 64
-SLOTS = 320
+PADS = 80
 KEYS = 256
 PAIR = 2 * HEAD_FEATURES
 SCALE = HEAD_FEATURES ** (-0.5)
@@ -289,10 +289,12 @@
     place = low + jnp.where(
         spot < span, spot, jnp.where(spot < span + HALO, spot - span - HALO, spot - HALO)
     )
+    slot = jnp.where((place >= start) & (place < end), place - start, -1)
+    own = low + lax.broadcasted_iota(jnp.int32, (1, span), 1)
     lead = jnp.maximum(start - before, 0)
-    slot = jnp.where((place >= end) & (place < after), IMAGE_TOKENS + lead + place - end, -1)
-    slot = jnp.where((place >= before) & (place < start), IMAGE_TOKENS + place - before, slot)
-    return jnp.where((place >= start) & (place < end), place - start, slot)
+    pad = jnp.where((own >= end) & (own < after), lead + own - end, -1)
+    pad = jnp.where((own >= before) & (own < start), own - before, pad)
+    return slot, pad
 
 
 def needed(tokens):
@@ -309,9 +311,9 @@
     w_down_hbm, b_down,
     out, tgr, pgr,
     w_qkv, w_out, w_up, w_down, w_sem,
-    prom, pick, ins, n1, inv1, wide, qkv, probs, turned, hid, n2, inv2, act, upg, og, grad,
+    prom, pick, pad_pick, pad_tok, ins, n1, inv1, wide, qkv, probs, turned, hid, n2, inv2, act, upg, og, grad,
     halos, halo_send, halo_recv, sides, backs, side_send, side_recv,
-    part, part_in, part_send, part_recv,
+    part, part_in, part_floor, summed, part_send, part_recv,
 ):
     index = lax.axis_index("seq")
     group = lax.axis_index("batch")
@@ -379,10 +381,35 @@
         result[r, :HALO] = result[r, :HALO] + backs[kind, r, :HALO]
         result[r, span - HALO :] = result[r, span - HALO :] + backs[kind, r, HALO:]
 
-    def flipped(place, step):
-        return place + step - 2 * step * (place // step % 2)
-
-    partners = tuple({"batch": flipped(group, k)} for k in (1, 2)) + tuple({"seq": flipped(index, k)} for k in (1, 2, 4))
+    down, deep = index // 2, index % 2
+    piece = group * 2 + deep
+    mates = []
+    for k in range(1, 8):
+        other = lax.rem(piece + k, 8)
+        mates.append((other, {"batch": other // 2, "seq": down * 2 + lax.rem(other, 2)}))
+    floors = [{"batch": group, "seq": lax.rem(down + k, 4) * 2 + deep} for k in range(1, 4)]
+
+    def eight(place):
+        return pl.ds(pl.multiple_of(place * 8, 8), 8)
+
+    def part_copy(k, source, target, device):
+        return pltpu.make_async_remote_copy(
+            source, target, part_send.at[k], part_recv.at[k], device_id=device, device_id_type=MESH
+        )
+
+    spread = [
+        part_copy(k, part.at[eight(other)], part_in.at[eight(piece)], device)
+        for k, (other, device) in enumerate(mates)
+    ]
+    climb = [
+        part_copy(7 + k, part_floor.at[eight(down)], part_floor.at[eight(down)], device)
+        for k, device in enumerate(floors)
+    ]
+    hand = [
+        part_copy(10 + k, summed.at[eight(piece)], summed.at[eight(piece)], device)
+        for k, (_, device) in enumerate(mates)
+    ]
+    partners = [device for _, device in mates] + floors
 
     @pl.when(row == 0)
     def _():
@@ -405,26 +432,25 @@
         pl.semaphore_wait(barrier, len(partners) + jnp.where(has_left, 1, 0) + jnp.where(has_right, 1, 0))
         halo_start(0, 0)
 
-    slot = slot_map(ids[pl.ds(row, 1)], index, span)
-    slots = lax.broadcasted_iota(jnp.int32, (SLOTS, span + 2 * HALO), 0)
+    slot, pad = slot_map(ids[pl.ds(row, 1)], index, span)
+    slots = lax.broadcasted_iota(jnp.int32, (KEYS, span + 2 * HALO), 0)
     pick[...] = jnp.where(slots == slot, 1.0, 0.0).astype(bf)
+    pads = lax.broadcasted_iota(jnp.int32, (PADS, span), 0)
+    pad_pick[row] = jnp.where(pads == pad, 1.0, 0.0).astype(bf)
+    pad_tok[row] = dot(pad_pick[row], tok[0]).astype(bf)
 
     first_rows = lax.broadcasted_iota(jnp.int32, (64, 1), 0)
     is_prompt = (first_rows >= 1) & (first_rows <= PROMPTS)
     halo_wait(0, row)
     halo_start(1, row)
-    for r in range(0, SLOTS, 64):
+    for r in range(0, KEYS, 64):
         x = dot(pick[r : r + 64, :span], tok[0]) + dot(pick[r : r + 64, span:], halos[0, row])
         if r == 0:
             x = jnp.where(is_prompt, prom[...], x)
         ins[r : r + 64] = x
-        mean = jnp.mean(x, axis=-1, keepdims=True)
-        c = x - mean
-        inv = lax.rsqrt(jnp.mean(c * c, axis=-1, keepdims=True) + 1e-06)
-        c = c * inv
-        if r < KEYS:
-            n1[r : r + 64] = c
-            inv1[r : r + 64] = inv
+        c, inv = normalize(x)
+        n1[r : r + 64] = c
+        inv1[r : r + 64] = inv
         wide[r : r + 64] = (c * g1[...][None] + b1[...][None]).astype(bf)
 
     arrived(0)
@@ -433,7 +459,7 @@
         qkv[:KEYS, c : c + 256] = (q * SCALE).astype(bf)
         k = dot(wide[:KEYS], w_qkv[:, width + c : width + c + 256])
         qkv[:KEYS, width + c : width + c + 256] = k.astype(bf)
-        v = dot(wide[...], w_qkv[:, 2 * width + c : 2 * width + c + 256]) + b_qv[width + c : width + c + 256][None]
+        v = dot(wide[:KEYS], w_qkv[:, 2 * width + c : 2 * width + c + 256]) + b_qv[width + c : width + c + 256][None]
         qkv[:, 2 * width + c : 2 * width + c + 256] = v.astype(bf)
 
     lane = lax.broadcasted_iota(jnp.int32, (1, PAIR), 1)
@@ -466,46 +492,36 @@
         turned[at : at + HEAD_FEATURES] = head0.astype(bf)
         turned[at + HEAD_FEATURES : at + PAIR] = head1.astype(bf)
 
-    key_rows = lax.broadcasted_iota(jnp.int32, (KEYS, 1), 0)
-    attended = turned[...].T
-    wide[:KEYS] = jnp.where(key_rows < IMAGE_TOKENS, attended, qkv[:KEYS, 2 * width :])
-    wide[KEYS:] = qkv[KEYS:, 2 * width :]
+    wide[:KEYS] = turned[...].T
     arrived(1)
     for c in range(0, width, 256):
-        hid[:, c : c + 256] = ins[:, c : c + 256] + dot(wide[...], w_out[:, c : c + 256]) + b_out[c : c + 256][None]
-
-    for r in range(0, SLOTS, 64):
-        x = hid[r : r + 64]
-        mean = jnp.mean(x, axis=-1, keepdims=True)
-        c = x - mean
-        inv = lax.rsqrt(jnp.mean(c * c, axis=-1, keepdims=True) + 1e-06)
-        c = c * inv
-        if r < KEYS:
-            n2[r : r + 64] = c
-            inv2[r : r + 64] = inv
+        hid[:KEYS, c : c + 256] = ins[:KEYS, c : c + 256] + dot(wide[:KEYS], w_out[:, c : c + 256]) + b_out[c : c + 256][None]
+
+    for r in range(0, KEYS, 64):
+        c, inv = normalize(hid[r : r + 64])
+        n2[r : r + 64] = c
+        inv2[r : r + 64] = inv
         wide[r : r + 64] = (c * g2[...][None] + b2[...][None]).astype(bf)
     halo_wait(1, row)
     pl.when(row < rows - 1)(lambda: halo_start(0, row + 1))
     for r in range(0, KEYS, 64):
         x = dot(pick[r : r + 64, :span], cot[0]) + dot(pick[r : r + 64, span:], halos[1, row])
-        if r + 64 == KEYS:
-            x = jnp.where(first_rows < IMAGE_TOKENS - r, x, 0.0)
         og[r : r + 64] = x.astype(bf)
 
     arrived(2)
     arrived(3)
     for c in range(0, ff, 256):
-        upper = dot(wide[...], w_up[:, c : c + 256]) + b_up[c : c + 256][None]
+        upper = dot(wide[:KEYS], w_up[:, c : c + 256]) + b_up[c : c + 256][None]
         act_grad = dot_nt(og[...], w_down[c : c + 256, :])
         value, slope = gelu_parts(upper)
-        act[:, c : c + 256] = value.astype(bf)
-        upg[:, c : c + 256] = (act_grad * slope[:KEYS]).astype(bf)
+        act[:KEYS, c : c + 256] = value.astype(bf)
+        upg[:, c : c + 256] = (act_grad * slope).astype(bf)
     for c in range(0, width, 256):
-        y = hid[:, c : c + 256] + dot(act[...], w_down[:, c : c + 256]) + b_down[c : c + 256][None]
-        wide[:, c : c + 256] = y.astype(bf)
+        y = hid[:KEYS, c : c + 256] + dot(act[:KEYS], w_down[:, c : c + 256]) + b_down[c : c + 256][None]
+        wide[:KEYS, c : c + 256] = y.astype(bf)
         grad[:, c : c + 256] = dot_nt(upg[...], w_up[c : c + 256, :])
-    out[row] = dot_tn(pick[:, :span], wide[...]).astype(bf)
-    sides[0, row] = dot_tn(pick[:, span:], wide[...]).astype(bf)
+    out[row] = dot_tn(pick[:, :span], wide[:KEYS]).astype(bf)
+    sides[0, row] = dot_tn(pick[:, span:], wide[:KEYS]).astype(bf)
 
     for r in range(0, KEYS, 64):
         e = grad[r : r + 64] * g2[...][None]
@@ -548,10 +564,16 @@
         x = hid[r : r + 64] + inv1[r : r + 64] * (e - mean - n * lean)
         if r == 0:
             part[...] += x
+
+            @pl.when(row == rows - 1)
+            def _():
+                for copy in spread:
+                    copy.start()
+
             x = jnp.where(is_prompt, 0.0, x)
         wide[r : r + 64] = x.astype(bf)
-    tgr[row] = dot_tn(pick[:KEYS, :span], wide[:KEYS]).astype(bf)
-    sides[1, row] = dot_tn(pick[:KEYS, span:], wide[:KEYS]).astype(bf)
+    tgr[row] = dot_tn(pick[:, :span], wide[:KEYS]).astype(bf)
+    sides[1, row] = dot_tn(pick[:, span:], wide[:KEYS]).astype(bf)
 
     @pl.when(row > 0)
     def _():
@@ -562,43 +584,55 @@
 
     @pl.when(row == rows - 1)
     def _():
-        def exchange(stage, source, target):
-            partner = partners[(0, 1, 2, 3, 4, 2, 1, 0)[stage]]
-            copy = pltpu.make_async_remote_copy(
-                source, target, part_send.at[stage], part_recv.at[stage], device_id=partner, device_id_type=MESH
-            )
+        many = rows * PADS
+        for r in range(rows):
+            ins[r * PADS : (r + 1) * PADS] = pad_tok[r].astype(jnp.float32)
+        for r in range(0, many, 64):
+            c, _ = normalize(ins[r : r + 64])
+            wide[r : r + 64] = (c * g1[...][None] + b1[...][None]).astype(bf)
+        for c in range(0, width, 256):
+            v = dot(wide[...], w_qkv[:, 2 * width + c : 2 * width + c + 256])
+            act[:, c : c + 256] = (v + b_qv[width + c : width + c + 256][None]).astype(bf)
+        for c in range(0, width, 256):
+            h = ins[:, c : c + 256] + dot(act[:, :width], w_out[:, c : c + 256])
+            hid[:, c : c + 256] = h + b_out[c : c + 256][None]
+        for r in range(0, many, 64):
+            c, _ = normalize(hid[r : r + 64])
+            wide[r : r + 64] = (c * g2[...][None] + b2[...][None]).astype(bf)
+
+        for copy in spread:
+            copy.wait_recv()
+        part_in[eight(piece)] = part[eight(piece)]
+        mine = part_in[0:8]
+        for k in range(8, 64, 8):
+            mine = mine + part_in[k : k + 8]
+        part_floor[eight(down)] = mine
+        for copy in climb:
             copy.start()
-            copy.wait()
-
-        def rows_at(first, size):
-            return pl.ds(pl.multiple_of(first, 8), size)
-
-        first = 0
-        size = part.shape[0]
-        kept = []
-        base = 0
-        for stage, bit in enumerate((group % 2, group // 2, index % 2)):
-            size = size // 2
-            kept.append((first, size, bit))
-            landed = part_in.at[base : base + size]
-            exchange(stage, part.at[rows_at(first + (1 - bit) * size, size)], landed)
-            first = first + bit * size
-            part[rows_at(first, size)] += landed[...]
-            base += size
-        for stage in (3, 4):
-            landed = part_in.at[base : base + size]
-            exchange(stage, part.at[rows_at(first, size)], landed)
-            part[rows_at(first, size)] += landed[...]
-            base += size
-        for stage in (5, 6, 7):
-            before, size, bit = kept[7 - stage]
-            landed = part_in.at[base : base + size]
-            exchange(stage, part.at[rows_at(before + bit * size, size)], landed)
-            part[rows_at(before + (1 - bit) * size, size)] = landed[...]
-            base += size
-        pgr[...] = part[1 : PROMPTS + 1]
+
+        for c in range(0, ff, 256):
+            upper = dot(wide[...], w_up[:, c : c + 256]) + b_up[c : c + 256][None]
+            act[:, c : c + 256] = gelu_parts(upper)[0].astype(bf)
+
+        for copy in climb:
+            copy.wait_recv()
+        summed[eight(piece)] = (part_floor[0:8] + part_floor[8:16]) + (part_floor[16:24] + part_floor[24:32])
+        for copy in hand:
+            copy.start()
+
+        for c in range(0, width, 256):
+            y = hid[:, c : c + 256] + dot(act[...], w_down[:, c : c + 256]) + b_down[c : c + 256][None]
+            wide[:, c : c + 256] = y.astype(bf)
+        for r in range(rows):
+            out[r] = out[r] + dot_tn(pad_pick[r], wide[r * PADS : (r + 1) * PADS]).astype(bf)
+
         side_merge(0, row)
         side_merge(1, row)
+        for copy in hand:
+            copy.wait_recv()
+        pgr[...] = summed[1 : PROMPTS + 1]
+        for copy in spread + climb + hand:
+            copy.wait_send()
         for r in range(rows):
             for kind in range(2):
                 sized(to_right, lambda size: halo_right(kind, r, size).wait_send())
@@ -641,16 +675,18 @@
         scratch_shapes=[
             pltpu.VMEM(w_qkv.shape, bf), pltpu.VMEM(w_out.shape, bf), pltpu.VMEM(w_up.shape, bf),
             pltpu.VMEM(w_down.shape, bf), dma((4,)),
-            pltpu.VMEM((64, width), f32), pltpu.VMEM((SLOTS, span + 2 * HALO), bf), pltpu.VMEM((SLOTS, width), f32),
-            pltpu.VMEM((KEYS, width), f32), pltpu.VMEM((KEYS, 1), f32), pltpu.VMEM((SLOTS, width), bf),
-            pltpu.VMEM((SLOTS, 3 * width), bf), pltpu.VMEM((width // PAIR, KEYS, 2 * KEYS), bf),
-            pltpu.VMEM((width, KEYS), bf), pltpu.VMEM((SLOTS, width), f32), pltpu.VMEM((KEYS, width), f32),
-            pltpu.VMEM((KEYS, 1), f32), pltpu.VMEM((SLOTS, ff), bf), pltpu.VMEM((KEYS, ff), bf),
+            pltpu.VMEM((64, width), f32), pltpu.VMEM((KEYS, span + 2 * HALO), bf), pltpu.VMEM((rows, PADS, span), bf),
+            pltpu.VMEM((rows, PADS, width), bf), pltpu.VMEM((rows * PADS, width), f32), pltpu.VMEM((KEYS, width), f32),
+            pltpu.VMEM((KEYS, 1), f32), pltpu.VMEM((rows * PADS, width), bf), pltpu.VMEM((KEYS, 3 * width), bf),
+            pltpu.VMEM((width // PAIR, KEYS, 2 * KEYS), bf), pltpu.VMEM((width, KEYS), bf),
+            pltpu.VMEM((rows * PADS, width), f32), pltpu.VMEM((KEYS, width), f32), pltpu.VMEM((KEYS, 1), f32),
+            pltpu.VMEM((rows * PADS, ff), bf), pltpu.VMEM((KEYS, ff), bf),
             pltpu.VMEM((KEYS, width), bf), pltpu.VMEM((KEYS, width), f32),
             pltpu.VMEM((2, rows, 2 * HALO, width), bf), dma((2, rows, 2)), dma((2, rows, 2)),
             pltpu.VMEM((2, rows, 2 * HALO, width), bf), pltpu.VMEM((2, rows, 2 * HALO, width), bf),
             dma((2, rows, 2)), dma((2, rows, 2)),
-            pltpu.VMEM((64, width), f32), pltpu.VMEM((128, width), f32), dma((8,)), dma((8,)),
+            pltpu.VMEM((64, width), f32), pltpu.VMEM((64, width), f32), pltpu.VMEM((32, width), f32),
+            pltpu.VMEM((64, width), f32), dma((17,)), dma((17,)),
         ],
         compiler_params=pltpu.CompilerParams(
             vmem_limit_bytes=62 << 20, dimension_semantics=("arbitrary",), collective_id=0, has_side_effects=True

time: 115 us -> 106 us (0.922)
  Pallas kernels: 110 us -> 101 us
    pallas_call x1, Pallas kernels: 110 us -> 101 us  [image_body(): pl.pallas_call(row_kernel, grid=(rows,), in_specs=[whole(image_id), per_r...]
where the time goes in v4:
time: 106 us
  Pallas kernels  101 us (95%)
  local copies, waits for them, and re-layouts  4.59 us (4%)
    pallas_call x1, Pallas kernels, image_body(): pl.pallas_call(row_kernel, grid=(rows,), in_specs=[whole(image_id), per_r...  101 us
    unnamed x7, local copies, waits for them, and re-layouts  4.59 us

profile of v4, /device:TPU:0, one launch (start us, length us, event | category | flops | bytes accessed | tf_op | source)
XLA Modules:
  0.0 106.2 jit_solution(7200047064754652017)
XLA Ops:
  0.6 100.9 %layer_rows.1 = (bf16[4,256,768]{2,1,0:T(8,128)(2,1)}, bf16[4,256,768]{2,1,0:T(8,128)(2,1)}, f32[50,768]{1,0:T(8,128)}) custom-call(s32[4,2048]{1,0:T(4,128)} %ids.1, bf16[4,256,768]{2,1,0:T(8,128)(2,1)} %tok_all.1, bf16[4,256,768]{2,1,0:T(8,128)(2,1)} %cot_all.1, bf16[4,256,768]{2,1,0:T(8,128)(2,1)} %tok_all.1, bf16[4,256,768]{2,1,0:T(8,128)(2,1)} %cot_all.1, ...), custom_call_target="tpu_custom_call" | custom-call | tf_op jit(solution)/shard_map/layer_rows/pallas_call | solution.py:659
  101.6 0.0 copy-start
  101.6 2.8 %copy.22 = bf16[4,256,768]{2,1,0:T(8,128)(2,1)} copy(bf16[4,256,768]{2,1,0:T(8,128)(2,1)} %get-tuple-element.6) | data formatting | bytes 3145728
  104.3 0.0 copy-done
  104.3 0.0 copy-start.1
  104.3 1.1 %copy.23 = bf16[4,256,768]{2,1,0:T(8,128)(2,1)} copy(bf16[4,256,768]{2,1,0:T(8,128)(2,1)S(1)} %copy-done) | data formatting | bytes 3145728
  105.5 0.0 copy-done.1
  105.5 0.7 copy.24
Async XLA Ops:
  101.6 2.8 %copy-start = (bf16[4,256,768]{2,1,0:T(8,128)(2,1)S(1)}, bf16[4,256,768]{2,1,0:T(8,128)(2,1)}, u32[]{:S(2)}) copy-start(bf16[4,256,768]{2,1,0:T(8,128)(2,1)} %get-tuple-element.7) | copy-start | bytes 4718596
  104.3 1.1 %copy-start.1 = (f32[50,768]{1,0:T(8,128)S(1)}, f32[50,768]{1,0:T(8,128)}, u32[]{:S(2)}) copy-start(f32[50,768]{1,0:T(8,128)} %get-tuple-element.8) | copy-start | bytes 460804

commit v5 on v4

--- a/solution.py
+++ b/solution.py
@@ -234,6 +234,7 @@
 MESH = pl.DeviceIdType.MESH
 HALO = 64
 PADS = 80
+CUTS = (4, 8)
 KEYS = 256
 PAIR = 2 * HEAD_FEATURES
 SCALE = HEAD_FEATURES ** (-0.5)
@@ -311,7 +312,7 @@
     w_down_hbm, b_down,
     out, tgr, pgr,
     w_qkv, w_out, w_up, w_down, w_sem,
-    prom, pick, pad_pick, pad_tok, ins, n1, inv1, wide, qkv, probs, turned, hid, n2, inv2, act, upg, og, grad,
+    prom, pick, pad_pick, pad_wide, pad_hid, ins, n1, inv1, wide, qkv, probs, turned, hid, n2, inv2, act, upg, og, grad,
     halos, halo_send, halo_recv, sides, backs, side_send, side_recv,
     part, part_in, part_floor, summed, part_send, part_recv,
 ):
@@ -334,9 +335,6 @@
         source = (w_qkv_hbm, w_out_hbm, w_up_hbm, w_down_hbm)[k]
         return pltpu.make_async_copy(source, (w_qkv, w_out, w_up, w_down)[k], w_sem.at[k])
 
-    def arrived(k):
-        pl.when(row == 0)(lambda: weight(k).wait())
-
     def seq_copy(source, target, send, recv, to):
         return pltpu.make_async_remote_copy(
             source, target, send, recv, device_id={"seq": to}, device_id_type=MESH
@@ -397,8 +395,9 @@
             source, target, part_send.at[k], part_recv.at[k], device_id=device, device_id_type=MESH
         )
 
+    pieces = PROMPTS // 8 + 1
     spread = [
-        part_copy(k, part.at[eight(other)], part_in.at[eight(piece)], device)
+        (other, part_copy(k, part.at[eight(other)], part_in.at[eight(piece)], device))
         for k, (other, device) in enumerate(mates)
     ]
     climb = [
@@ -410,10 +409,11 @@
         for k, (_, device) in enumerate(mates)
     ]
     partners = [device for _, device in mates] + floors
+    senders = [lax.rem(piece + 8 - k, 8) for k in range(1, 8)]
 
     @pl.when(row == 0)
     def _():
-        for k in range(4):
+        for k in range(2):
             weight(k).start()
         halos[...] = jnp.zeros_like(halos)
         backs[...] = jnp.zeros_like(backs)
@@ -431,20 +431,57 @@
         part[...] = jnp.zeros_like(part)
         pl.semaphore_wait(barrier, len(partners) + jnp.where(has_left, 1, 0) + jnp.where(has_right, 1, 0))
         halo_start(0, 0)
-
-    slot, pad = slot_map(ids[pl.ds(row, 1)], index, span)
+        halo_start(1, 0)
+        many = rows * PADS
+        for r in range(rows):
+            pads = lax.broadcasted_iota(jnp.int32, (PADS, span), 0)
+            pad_pick[r] = jnp.where(pads == slot_map(ids[r : r + 1], index, span)[1], 1.0, 0.0).astype(bf)
+            ins[r * PADS : (r + 1) * PADS] = dot(pad_pick[r], tok[r])
+        for r in range(0, many, 64):
+            c, _ = normalize(ins[r : r + 64])
+            wide[r : r + 64] = (c * g1[...][None] + b1[...][None]).astype(bf)
+        weight(0).wait()
+        for c in range(0, width, 256):
+            v = dot(wide[...], w_qkv[:, 2 * width + c : 2 * width + c + 256])
+            act[:, c : c + 256] = (v + b_qv[width + c : width + c + 256][None]).astype(bf)
+        weight(1).wait()
+        for k in range(2, 4):
+            weight(k).start()
+        for c in range(0, width, 256):
+            h = ins[:, c : c + 256] + dot(act[:, :width], w_out[:, c : c + 256])
+            pad_hid[:, c : c + 256] = h + b_out[c : c + 256][None]
+        for r in range(0, many, 64):
+            c, _ = normalize(pad_hid[r : r + 64])
+            pad_wide[r : r + 64] = (c * g2[...][None] + b2[...][None]).astype(bf)
+        for k in range(2, 4):
+            weight(k).wait()
+
+    halo_wait(0, row)
+    halo_wait(1, row)
+
+    @pl.when(row < rows - 1)
+    def _():
+        halo_start(0, row + 1)
+        halo_start(1, row + 1)
+
+    @pl.when(row > 0)
+    def _():
+        side_start(0, row - 1)
+        side_start(1, row - 1)
+
+    @pl.when(row > 1)
+    def _():
+        side_merge(0, row - 2)
+        side_merge(1, row - 2)
+
+    slot, _ = slot_map(ids[pl.ds(row, 1)], index, span)
     slots = lax.broadcasted_iota(jnp.int32, (KEYS, span + 2 * HALO), 0)
     pick[...] = jnp.where(slots == slot, 1.0, 0.0).astype(bf)
-    pads = lax.broadcasted_iota(jnp.int32, (PADS, span), 0)
-    pad_pick[row] = jnp.where(pads == pad, 1.0, 0.0).astype(bf)
-    pad_tok[row] = dot(pad_pick[row], tok[0]).astype(bf)
 
     first_rows = lax.broadcasted_iota(jnp.int32, (64, 1), 0)
     is_prompt = (first_rows >= 1) & (first_rows <= PROMPTS)
-    halo_wait(0, row)
-    halo_start(1, row)
     for r in range(0, KEYS, 64):
-        x = dot(pick[r : r + 64, :span], tok[0]) + dot(pick[r : r + 64, span:], halos[0, row])
+        x = dot(pick[r : r + 64, :span], tok[row]) + dot(pick[r : r + 64, span:], halos[0, row])
         if r == 0:
             x = jnp.where(is_prompt, prom[...], x)
         ins[r : r + 64] = x
@@ -453,7 +490,6 @@
         inv1[r : r + 64] = inv
         wide[r : r + 64] = (c * g1[...][None] + b1[...][None]).astype(bf)
 
-    arrived(0)
     for c in range(0, width, 256):
         q = dot(wide[:KEYS], w_qkv[:, c : c + 256]) + b_qv[c : c + 256][None]
         qkv[:KEYS, c : c + 256] = (q * SCALE).astype(bf)
@@ -493,7 +529,6 @@
         turned[at + HEAD_FEATURES : at + PAIR] = head1.astype(bf)
 
     wide[:KEYS] = turned[...].T
-    arrived(1)
     for c in range(0, width, 256):
         hid[:KEYS, c : c + 256] = ins[:KEYS, c : c + 256] + dot(wide[:KEYS], w_out[:, c : c + 256]) + b_out[c : c + 256][None]
 
@@ -502,14 +537,10 @@
         n2[r : r + 64] = c
         inv2[r : r + 64] = inv
         wide[r : r + 64] = (c * g2[...][None] + b2[...][None]).astype(bf)
-    halo_wait(1, row)
-    pl.when(row < rows - 1)(lambda: halo_start(0, row + 1))
     for r in range(0, KEYS, 64):
         x = dot(pick[r : r + 64, :span], cot[0]) + dot(pick[r : r + 64, span:], halos[1, row])
         og[r : r + 64] = x.astype(bf)
 
-    arrived(2)
-    arrived(3)
     for c in range(0, ff, 256):
         upper = dot(wide[:KEYS], w_up[:, c : c + 256]) + b_up[c : c + 256][None]
         act_grad = dot_nt(og[...], w_down[c : c + 256, :])
@@ -533,8 +564,6 @@
         wide[r : r + 64] = h.astype(bf)
     for c in range(0, width, 256):
         og[:, c : c + 256] = dot_nt(wide[:KEYS], w_out[c : c + 256, :]).astype(bf)
-
-    side_start(0, row)
 
     for p in range(width // PAIR):
         at = p * PAIR
@@ -564,75 +593,70 @@
         x = hid[r : r + 64] + inv1[r : r + 64] * (e - mean - n * lean)
         if r == 0:
             part[...] += x
-
-            @pl.when(row == rows - 1)
-            def _():
-                for copy in spread:
-                    copy.start()
-
             x = jnp.where(is_prompt, 0.0, x)
         wide[r : r + 64] = x.astype(bf)
+    @pl.when(row == rows - 1)
+    def _():
+        for other, copy in spread:
+            pl.when(other < pieces)(copy.start)
+
     tgr[row] = dot_tn(pick[:, :span], wide[:KEYS]).astype(bf)
     sides[1, row] = dot_tn(pick[:, span:], wide[:KEYS]).astype(bf)
 
-    @pl.when(row > 0)
-    def _():
-        side_merge(0, row - 1)
-        side_merge(1, row - 1)
-
-    side_start(1, row)
-
     @pl.when(row == rows - 1)
     def _():
-        many = rows * PADS
-        for r in range(rows):
-            ins[r * PADS : (r + 1) * PADS] = pad_tok[r].astype(jnp.float32)
-        for r in range(0, many, 64):
-            c, _ = normalize(ins[r : r + 64])
-            wide[r : r + 64] = (c * g1[...][None] + b1[...][None]).astype(bf)
+        side_start(0, row)
+        side_start(1, row)
+
+        def pad_up(first, last):
+            for c in range(first * 256, last * 256, 256):
+                upper = dot(pad_wide[...], w_up[:, c : c + 256]) + b_up[c : c + 256][None]
+                act[:, c : c + 256] = gelu_parts(upper)[0].astype(bf)
+
+        chunks = ff // 256
+        pad_up(0, chunks * CUTS[0] // 12)
+        @pl.when(piece < pieces)
+        def _():
+            for _, copy in spread:
+                copy.wait_recv()
+            part_in[eight(piece)] = part[eight(piece)]
+            mine = part_in[0:8]
+            for k in range(8, 64, 8):
+                mine = mine + part_in[k : k + 8]
+            part_floor[eight(down)] = mine
+            for copy in climb:
+                copy.start()
+
+        pad_up(chunks * CUTS[0] // 12, chunks * CUTS[1] // 12)
+        @pl.when(piece < pieces)
+        def _():
+            for copy in climb:
+                copy.wait_recv()
+            summed[eight(piece)] = (part_floor[0:8] + part_floor[8:16]) + (part_floor[16:24] + part_floor[24:32])
+            for copy in hand:
+                copy.start()
+
+        pad_up(chunks * CUTS[1] // 12, chunks)
         for c in range(0, width, 256):
-            v = dot(wide[...], w_qkv[:, 2 * width + c : 2 * width + c + 256])
-            act[:, c : c + 256] = (v + b_qv[width + c : width + c + 256][None]).astype(bf)
-        for c in range(0, width, 256):
-            h = ins[:, c : c + 256] + dot(act[:, :width], w_out[:, c : c + 256])
-            hid[:, c : c + 256] = h + b_out[c : c + 256][None]
-        for r in range(0, many, 64):
-            c, _ = normalize(hid[r : r + 64])
-            wide[r : r + 64] = (c * g2[...][None] + b2[...][None]).astype(bf)
-
-        for copy in spread:
-            copy.wait_recv()
-        part_in[eight(piece)] = part[eight(piece)]
-        mine = part_in[0:8]
-        for k in range(8, 64, 8):
-            mine = mine + part_in[k : k + 8]
-        part_floor[eight(down)] = mine
-        for copy in climb:
-            copy.start()
-
-        for c in range(0, ff, 256):
-            upper = dot(wide[...], w_up[:, c : c + 256]) + b_up[c : c + 256][None]
-            act[:, c : c + 256] = gelu_parts(upper)[0].astype(bf)
-
-        for copy in climb:
-            copy.wait_recv()
-        summed[eight(piece)] = (part_floor[0:8] + part_floor[8:16]) + (part_floor[16:24] + part_floor[24:32])
-        for copy in hand:
-            copy.start()
-
-        for c in range(0, width, 256):
-            y = hid[:, c : c + 256] + dot(act[...], w_down[:, c : c + 256]) + b_down[c : c + 256][None]
+            y = pad_hid[:, c : c + 256] + dot(act[...], w_down[:, c : c + 256]) + b_down[c : c + 256][None]
             wide[:, c : c + 256] = y.astype(bf)
         for r in range(rows):
             out[r] = out[r] + dot_tn(pad_pick[r], wide[r * PADS : (r + 1) * PADS]).astype(bf)
 
-        side_merge(0, row)
-        side_merge(1, row)
-        for copy in hand:
-            copy.wait_recv()
+        for r in (rows - 2, rows - 1):
+            side_merge(0, r)
+            side_merge(1, r)
+        for back, copy in zip(senders, hand):
+            pl.when(back < pieces)(copy.wait_recv)
         pgr[...] = summed[1 : PROMPTS + 1]
-        for copy in spread + climb + hand:
-            copy.wait_send()
+        for other, copy in spread:
+            pl.when(other < pieces)(copy.wait_send)
+
+        @pl.when(piece < pieces)
+        def _():
+            for copy in climb + hand:
+                copy.wait_send()
+
         for r in range(rows):
             for kind in range(2):
                 sized(to_right, lambda size: halo_right(kind, r, size).wait_send())
@@ -660,23 +684,19 @@
         row_kernel,
         grid=(rows,),
         in_specs=[
-            whole(image_id), per_row, per_row, in_place, in_place, whole(prompts), whole(ln1_gain), whole(ln1_bias),
+            whole(image_id), whole(tokens), per_row, in_place, in_place, whole(prompts), whole(ln1_gain), whole(ln1_bias),
             in_place, whole(bias_qv), in_place, whole(bias_out), whole(ln2_gain), whole(ln2_bias), in_place,
             whole(bias_up), in_place, whole(bias_down),
         ],
-        out_specs=[
-            pl.BlockSpec((rows, span, width), lambda r: (0, 0, 0)), pl.BlockSpec((rows, span, width), lambda r: (0, 0, 0)),
-            pl.BlockSpec((PROMPTS, width), lambda r: (0, 0)),
-        ],
+        out_specs=[pl.BlockSpec(memory_space=pltpu.VMEM)] * 3,
         out_shape=[
-            jax.ShapeDtypeStruct((rows, span, width), bf), jax.ShapeDtypeStruct((rows, span, width), bf),
-            jax.ShapeDtypeStruct((PROMPTS, width), f32),
+            pltpu.VMEM((rows, span, width), bf), pltpu.VMEM((rows, span, width), bf), pltpu.VMEM((PROMPTS, width), f32),
         ],
         scratch_shapes=[
             pltpu.VMEM(w_qkv.shape, bf), pltpu.VMEM(w_out.shape, bf), pltpu.VMEM(w_up.shape, bf),
             pltpu.VMEM(w_down.shape, bf), dma((4,)),
             pltpu.VMEM((64, width), f32), pltpu.VMEM((KEYS, span + 2 * HALO), bf), pltpu.VMEM((rows, PADS, span), bf),
-            pltpu.VMEM((rows, PADS, width), bf), pltpu.VMEM((rows * PADS, width), f32), pltpu.VMEM((KEYS, width), f32),
+            pltpu.VMEM((rows * PADS, width), bf), pltpu.VMEM((rows * PADS, width), f32), pltpu.VMEM((rows * PADS, width), f32), pltpu.VMEM((KEYS, width), f32),
             pltpu.VMEM((KEYS, 1), f32), pltpu.VMEM((rows * PADS, width), bf), pltpu.VMEM((KEYS, 3 * width), bf),
             pltpu.VMEM((width // PAIR, KEYS, 2 * KEYS), bf), pltpu.VMEM((width, KEYS), bf),
             pltpu.VMEM((rows * PADS, width), f32), pltpu.VMEM((KEYS, width), f32), pltpu.VMEM((KEYS, 1), f32),
@@ -689,7 +709,7 @@
             pltpu.VMEM((64, width), f32), dma((17,)), dma((17,)),
         ],
         compiler_params=pltpu.CompilerParams(
-            vmem_limit_bytes=62 << 20, dimension_semantics=("arbitrary",), collective_id=0, has_side_effects=True
+            vmem_limit_bytes=56 << 20, dimension_semantics=("arbitrary",), collective_id=0, has_side_effects=True
         ),
         name="layer_rows",
     )(

time: 106 us -> 100 us (0.943)
  Pallas kernels: 101 us -> 96.3 us
  local copies, waits for them, and re-layouts: 4.59 us -> 2.96 us
    pallas_call x1, Pallas kernels: 101 us -> 96.3 us  [image_body(): pl.pallas_call(row_kernel, grid=(rows,), in_specs=[whole(image_id), whole...]
    unnamed x7 -> x3, local copies, waits for them, and re-layouts: 4.59 us -> 2.96 us
where the time goes in v5:
time: 100 us; the launch traced here: 99.9 us
  Pallas kernels  96.3 us (96%)
  local copies, waits for them, and re-layouts  2.96 us (3%)
    pallas_call x1, Pallas kernels, image_body(): pl.pallas_call(row_kernel, grid=(rows,), in_specs=[whole(image_id), whole...  96.3 us
    unnamed x3, local copies, waits for them, and re-layouts  2.96 us

profile of v5, /device:TPU:0, one launch (start us, length us, event | category | flops | bytes accessed | tf_op | source)
XLA Modules:
  0.0 99.9 jit_solution(6070099164821417432)
XLA Ops:
  0.6 96.3 %layer_rows.1 = (bf16[4,256,768]{2,1,0:T(8,128)(2,1)S(1)}, bf16[4,256,768]{2,1,0:T(8,128)(2,1)S(1)}, f32[50,768]{1,0:T(8,128)S(1)}) custom-call(s32[4,2048]{1,0:T(4,128)} %ids.1, bf16[4,256,768]{2,1,0:T(8,128)(2,1)} %tok_all.1, bf16[4,256,768]{2,1,0:T(8,128)(2,1)} %cot_all.1, bf16[4,256,768]{2,1,0:T(8,128)(2,1)} %tok_all.1, bf16[4,256,768]{2,1,0:T(8,128)(2,1)} %cot_all.1, ...), custom_call_target="tpu_custom_call" | custom-call | tf_op jit(solution)/shard_map/layer_rows/pallas_call | solution.py:683
  96.9 1.1 %copy.22 = bf16[4,256,768]{2,1,0:T(8,128)(2,1)} copy(bf16[4,256,768]{2,1,0:T(8,128)(2,1)S(1)} %get-tuple-element.3) | data formatting | bytes 3145728
  98.1 0.7 copy.24
  98.7 1.1 %copy.23 = bf16[4,256,768]{2,1,0:T(8,128)(2,1)} copy(bf16[4,256,768]{2,1,0:T(8,128)(2,1)S(1)} %get-tuple-element.4) | data formatting | bytes 3145728

commit v6 on v5

--- a/solution.py
+++ b/solution.py
@@ -314,7 +314,7 @@
     w_qkv, w_out, w_up, w_down, w_sem,
     prom, pick, pad_pick, pad_wide, pad_hid, ins, n1, inv1, wide, qkv, probs, turned, hid, n2, inv2, act, upg, og, grad,
     halos, halo_send, halo_recv, sides, backs, side_send, side_recv,
-    part, part_in, part_floor, summed, part_send, part_recv,
+    part, part_low, part_in, part_floor, summed, part_send, part_recv,
 ):
     index = lax.axis_index("seq")
     group = lax.axis_index("batch")
@@ -397,15 +397,15 @@
 
     pieces = PROMPTS // 8 + 1
     spread = [
-        (other, part_copy(k, part.at[eight(other)], part_in.at[eight(piece)], device))
+        (other, part_copy(k, part_low.at[other], part_in.at[piece], device))
         for k, (other, device) in enumerate(mates)
     ]
     climb = [
-        part_copy(7 + k, part_floor.at[eight(down)], part_floor.at[eight(down)], device)
+        part_copy(7 + k, part_floor.at[down], part_floor.at[down], device)
         for k, device in enumerate(floors)
     ]
     hand = [
-        part_copy(10 + k, summed.at[eight(piece)], summed.at[eight(piece)], device)
+        part_copy(10 + k, summed.at[piece], summed.at[piece], device)
         for k, (_, device) in enumerate(mates)
     ]
     partners = [device for _, device in mates] + floors
@@ -457,7 +457,7 @@
             weight(k).wait()
 
     halo_wait(0, row)
-    halo_wait(1, row)
+    pl.when(row > 0)(lambda: halo_wait(1, row))
 
     @pl.when(row < rows - 1)
     def _():
@@ -537,6 +537,7 @@
         n2[r : r + 64] = c
         inv2[r : r + 64] = inv
         wide[r : r + 64] = (c * g2[...][None] + b2[...][None]).astype(bf)
+    pl.when(row == 0)(lambda: halo_wait(1, row))
     for r in range(0, KEYS, 64):
         x = dot(pick[r : r + 64, :span], cot[0]) + dot(pick[r : r + 64, span:], halos[1, row])
         og[r : r + 64] = x.astype(bf)
@@ -597,6 +598,8 @@
         wide[r : r + 64] = x.astype(bf)
     @pl.when(row == rows - 1)
     def _():
+        for k in range(8):
+            part_low[k] = part[8 * k : 8 * k + 8].astype(bf)
         for other, copy in spread:
             pl.when(other < pieces)(copy.start)
 
@@ -619,11 +622,11 @@
         def _():
             for _, copy in spread:
                 copy.wait_recv()
-            part_in[eight(piece)] = part[eight(piece)]
-            mine = part_in[0:8]
-            for k in range(8, 64, 8):
-                mine = mine + part_in[k : k + 8]
-            part_floor[eight(down)] = mine
+            part_in[piece] = jnp.zeros_like(part_in[piece])
+            mine = part[eight(piece)]
+            for k in range(8):
+                mine = mine + part_in[k].astype(jnp.float32)
+            part_floor[down] = mine.astype(bf)
             for copy in climb:
                 copy.start()
 
@@ -632,7 +635,8 @@
         def _():
             for copy in climb:
                 copy.wait_recv()
-            summed[eight(piece)] = (part_floor[0:8] + part_floor[8:16]) + (part_floor[16:24] + part_floor[24:32])
+            level = [part_floor[k].astype(jnp.float32) for k in range(4)]
+            summed[piece] = ((level[0] + level[1]) + (level[2] + level[3])).astype(bf)
             for copy in hand:
                 copy.start()
 
@@ -648,7 +652,9 @@
             side_merge(1, r)
         for back, copy in zip(senders, hand):
             pl.when(back < pieces)(copy.wait_recv)
-        pgr[...] = summed[1 : PROMPTS + 1]
+        for k in range(pieces):
+            part[8 * k : 8 * k + 8] = summed[k].astype(jnp.float32)
+        pgr[...] = part[1 : PROMPTS + 1]
         for other, copy in spread:
             pl.when(other < pieces)(copy.wait_send)
 
@@ -705,8 +711,8 @@
             pltpu.VMEM((2, rows, 2 * HALO, width), bf), dma((2, rows, 2)), dma((2, rows, 2)),
             pltpu.VMEM((2, rows, 2 * HALO, width), bf), pltpu.VMEM((2, rows, 2 * HALO, width), bf),
             dma((2, rows, 2)), dma((2, rows, 2)),
-            pltpu.VMEM((64, width), f32), pltpu.VMEM((64, width), f32), pltpu.VMEM((32, width), f32),
-            pltpu.VMEM((64, width), f32), dma((17,)), dma((17,)),
+            pltpu.VMEM((64, width), f32), pltpu.VMEM((8, 8, width), bf), pltpu.VMEM((8, 8, width), bf),
+            pltpu.VMEM((4, 8, width), bf), pltpu.VMEM((8, 8, width), bf), dma((17,)), dma((17,)),
         ],
         compiler_params=pltpu.CompilerParams(
             vmem_limit_bytes=56 << 20, dimension_semantics=("arbitrary",), collective_id=0, has_side_effects=True

time: 100 us -> 99 us (0.990)
  Pallas kernels: 96.3 us -> 95.2 us
    pallas_call x1, Pallas kernels: 96.3 us -> 95.2 us  [image_body(): pl.pallas_call(row_kernel, grid=(rows,), in_specs=[whole(image_id), whole...]
where the time goes in v6:
time: 99 us; the launch traced here: 98.8 us
  Pallas kernels  95.2 us (96%)
  local copies, waits for them, and re-layouts  2.96 us (3%)
    pallas_call x1, Pallas kernels, image_body(): pl.pallas_call(row_kernel, grid=(rows,), in_specs=[whole(image_id), whole...  95.2 us
    unnamed x3, local copies, waits for them, and re-layouts  2.96 us

profile of v6, /device:TPU:0, one launch (start us, length us, event | category | flops | bytes accessed | tf_op | source)
XLA Modules:
  0.0 98.8 jit_solution(7983710756986877741)
XLA Ops:
  0.6 95.2 %layer_rows.1 = (bf16[4,256,768]{2,1,0:T(8,128)(2,1)S(1)}, bf16[4,256,768]{2,1,0:T(8,128)(2,1)S(1)}, f32[50,768]{1,0:T(8,128)S(1)}) custom-call(s32[4,2048]{1,0:T(4,128)} %ids.1, bf16[4,256,768]{2,1,0:T(8,128)(2,1)} %tok_all.1, bf16[4,256,768]{2,1,0:T(8,128)(2,1)} %cot_all.1, bf16[4,256,768]{2,1,0:T(8,128)(2,1)} %tok_all.1, bf16[4,256,768]{2,1,0:T(8,128)(2,1)} %cot_all.1, ...), custom_call_target="tpu_custom_call" | custom-call | tf_op jit(solution)/shard_map/layer_rows/pallas_call | solution.py:689
  95.9 1.1 %copy.22 = bf16[4,256,768]{2,1,0:T(8,128)(2,1)} copy(bf16[4,256,768]{2,1,0:T(8,128)(2,1)S(1)} %get-tuple-element.3) | data formatting | bytes 3145728
  97.0 0.7 copy.24
  97.7 1.1 %copy.23 = bf16[4,256,768]{2,1,0:T(8,128)(2,1)} copy(bf16[4,256,768]{2,1,0:T(8,128)(2,1)S(1)} %get-tuple-element.4) | data formatting | bytes 3145728
